TPU v7x, 8 devices: a whole 2x2x1 slice. The times are simulated.
8 devices in a mesh: dp: 1 (over z), tp: 8 (over y, x, core).
Axes of the slice: x: 2, y: 2, z: 1, core: 2. Of those that a mesh axis runs over, the one named last changes fastest.
Arguments:
- x_in: bfloat16 [1024, 6144], P(('dp', 'tp'))
- dy_in: bfloat16 [1024, 6144], P(('dp', 'tp'))
- w_q: bfloat16 [6144, 48, 128], P(None, 'tp')
- w_k: bfloat16 [6144, 1, 128], replicated
- w_v: bfloat16 [6144, 1, 128], replicated
- w_o: bfloat16 [48, 128, 6144], P('tp')
Outputs:
- output 1: bfloat16 [1024, 6144], P(('dp', 'tp'))
- output 2: float32 [6144, 48, 128], P('dp', 'tp')
- output 3: float32 [48, 128, 6144], P(('dp', 'tp'))
- output 4: float32 [6144, 128], P(('dp', 'tp'))
- output 5: float32 [6144, 128], P(('dp', 'tp'))
All inputs are finite; a program needn't handle non-finite values.
Results may differ from a plain program's by a relative error of at most 0.00989535.
Values are sent between devices in bfloat16 or wider.
A program may use at most 1 GiB of HBM per device.

v0:
```python
import jax
import jax.numpy as jnp
from jax import lax
from jax.sharding import PartitionSpec as P


def solution(mesh):
    n_model = mesh.shape["tp"]

    def local_grads(x_blk, dy_blk, wq_loc, w_k, w_v, wo_loc):
        f32 = jnp.float32
        bf16 = jnp.bfloat16
        model_dim, kv_heads, head_dim = w_k.shape
        repl = n_model // kv_heads
        scale = head_dim ** -0.5
        dev_idx = lax.axis_index("tp")
        kv_index = dev_idx // repl
        wk_loc = lax.dynamic_index_in_dim(w_k, kv_index, axis=1, keepdims=False)
        wv_loc = lax.dynamic_index_in_dim(w_v, kv_index, axis=1, keepdims=False)
        x_full = lax.all_gather(x_blk, "tp", axis=0, tiled=True)
        dy_full = lax.all_gather(dy_blk, "tp", axis=0, tiled=True)
        tokens = x_full.shape[0]
        queries = jnp.einsum("tc,che->hte", x_full, wq_loc, preferred_element_type=f32).astype(bf16)
        key_rows = jnp.dot(x_full, wk_loc, preferred_element_type=f32).astype(bf16)
        val_rows = jnp.dot(x_full, wv_loc, preferred_element_type=f32).astype(bf16)
        causal = lax.broadcasted_iota(jnp.int32, (tokens, tokens), 0) >= lax.broadcasted_iota(jnp.int32, (tokens, tokens), 1)
        scores = jnp.einsum("hqe,ke->hqk", queries, key_rows, preferred_element_type=f32) * scale
        scores = jnp.where(causal, scores, -jnp.inf)
        attn_prob = jax.nn.softmax(scores, axis=-1)
        prob_bf = attn_prob.astype(bf16)
        attn_out = jnp.einsum("hqk,ke->hqe", prob_bf, val_rows, preferred_element_type=f32).astype(bf16)
        d_out = jnp.einsum("tc,hec->hte", dy_full, wo_loc, preferred_element_type=f32).astype(bf16)
        grad_wo = jnp.einsum("hte,tc->hec", attn_out, dy_full, preferred_element_type=f32)
        d_prob = jnp.einsum("hqe,ke->hqk", d_out, val_rows, preferred_element_type=f32)
        delta_row = jnp.einsum("hqe,hqe->hq", d_out, attn_out, preferred_element_type=f32)[..., None]
        d_score = (attn_prob * (d_prob - delta_row)).astype(bf16)
        d_query = (jnp.einsum("hqk,ke->hqe", d_score, key_rows, preferred_element_type=f32) * scale).astype(bf16)
        d_key = (jnp.einsum("hqk,hqe->ke", d_score, queries, preferred_element_type=f32) * scale).astype(bf16)
        d_val = jnp.einsum("hqk,hqe->ke", prob_bf, d_out, preferred_element_type=f32).astype(bf16)
        grad_wq = jnp.einsum("tc,hte->che", x_full, d_query, preferred_element_type=f32)
        dx_part = (jnp.einsum("hte,che->tc", d_query, wq_loc, preferred_element_type=f32)
                   + jnp.einsum("te,ce->tc", d_key, wk_loc, preferred_element_type=f32)
                   + jnp.einsum("te,ce->tc", d_val, wv_loc, preferred_element_type=f32))
        dx_blk = lax.psum_scatter(dx_part, "tp", scatter_dimension=0, tiled=True).astype(bf16)
        slot = (jnp.arange(kv_heads) == kv_index)[:, None, None]
        wk_part = jnp.einsum("tc,te->ce", x_full, d_key, preferred_element_type=f32)
        wv_part = jnp.einsum("tc,te->ce", x_full, d_val, preferred_element_type=f32)
        wk_buf = jnp.where(slot, wk_part[None], 0.0).reshape(kv_heads * model_dim, head_dim)
        wv_buf = jnp.where(slot, wv_part[None], 0.0).reshape(kv_heads * model_dim, head_dim)
        dwk_blk = lax.psum_scatter(wk_buf, "tp", scatter_dimension=0, tiled=True)
        dwv_blk = lax.psum_scatter(wv_buf, "tp", scatter_dimension=0, tiled=True)
        return dx_blk, grad_wq, grad_wo, dwk_blk, dwv_blk

    tok_spec = P(("dp", "tp"))
    return jax.shard_map(
        local_grads,
        mesh=mesh,
        in_specs=(tok_spec, tok_spec, P(None, "tp", None), P(), P(), P("tp")),
        out_specs=(tok_spec, P("dp", "tp", None), tok_spec, tok_spec, tok_spec),
        check_vma=False,
    )
```

profile of v0, /device:TPU:0, one launch (start us, length us, event | category | flops | bytes accessed | tf_op | source)
XLA Modules:
  0.0 478.0 jit_solution(11067965916754572875)
XLA Ops:
  7.2 0.7 all-gather.5.cloned.1.call-update
  8.0 0.7 all-gather.3.cloned.1.call-update
  8.7 0.3 iota_compare_fusion
  9.0 69.9 %all-gather.5.cloned.1.call-done = bf16[1024,6144]{1,0:T(8,128)(2,1)} async-done(((bf16[128,6144]{1,0:T(8,128)(2,1)}), bf16[1024,6144]{1,0:T(8,128)(2,1)}) %all-gather.5.cloned.1.call-update) | async-done | bytes 12582928 | tf_op jit(solution)/shard_map/all_gather | solution.py:21
  79.0 17.1 %bitcast_convert_fusion = (f32[6,1024,128]{1,2,0:T(8,128)}, bf16[6,128,1024]{2,1,0:T(8,128)(2,1)}) fusion(bf16[6,128,6144]{2,1,0:T(8,128)(2,1)} %param.11, bf16[1024,6144]{1,0:T(8,128)(2,1)} %all-gather.5.cloned.1.call-done), kind=kOutput, calls=%fused_computation.38 | convolution fusion | flops 9665249280 | bytes 26738688 | tf_op jit(solution)/shard_map/tc,hec->hte/dot_general | solution.py:32
  96.0 3.5 copy.32
  99.6 47.5 %all-gather.3.cloned.1.call-done = bf16[1024,6144]{1,0:T(8,128)(2,1)} async-done(((bf16[128,6144]{1,0:T(8,128)(2,1)}), bf16[1024,6144]{1,0:T(8,128)(2,1)}) %all-gather.3.cloned.1.call-update) | async-done | bytes 12582928 | tf_op jit(solution)/shard_map/all_gather | solution.py:20
  147.1 16.3 %fusion.22 = bf16[6,128,1024]{2,1,0:T(8,128)(2,1)} fusion(bf16[6144,6,128]{2,0,1:T(8,128)(2,1)} %param.8, bf16[1024,6144]{1,0:T(8,128)(2,1)} %all-gather.3.cloned.1.call-done), kind=kOutput, calls=%fused_computation.30 | convolution fusion | flops 9664462848 | bytes 23592960 | tf_op jit(solution)/shard_map/tc,che->hte/dot_general | solution.py:23
  163.5 3.4 fusion.72
  166.9 14.6 %fusion.77 = (f32[6,1024]{1,0:T(8,128)S(1)}, f32[6,1024,1024]{1,2,0:T(8,128)}) fusion(pred[1024,1024]{0,1:T(8,128)(4,1)S(1)} %iota_compare_fusion, bf16[1024,128,1]{1,0,2:T(8,128)(2,1)S(1)} %fusion.72, bf16[6,128,1024]{2,1,0:T(8,128)(2,1)} %fusion.22), kind=kOutput, calls=%fused_computation.60 | convolution fusion | flops 1635779584 | bytes 28073984 | tf_op jit(solution)/shard_map/sub | solution.py:29
  181.5 10.2 %fusion.17 = bf16[6,1024,1024]{1,2,0:T(8,128)(2,1)S(1)} fusion(f32[6,1024,1024]{1,2,0:T(8,128)} %get-tuple-element.11, f32[6,1024]{1,0:T(8,128)S(1)} %get-tuple-element.10), kind=kLoop, calls=%fused_computation.20 | loop fusion | flops 12582912 | bytes 37773312 | tf_op jit(solution)/shard_map/convert_element_type | solution.py:30
  191.8 11.2 %fusion.69 = bf16[1024,128,1]{1,0,2:T(8,128)(2,1)S(1)} fusion(bf16[1024,6144]{1,0:T(8,128)(2,1)} %all-gather.3.cloned.1.call-done, bf16[6144,1,128]{2,0,1:T(8,128)(2,1)S(1)} %copy-done.4), kind=kOutput, calls=%fused_computation.56 | convolution fusion | flops 1610743808 | bytes 14417920 | tf_op jit(solution)/shard_map/dot_general | solution.py:25
  203.0 5.1 %multiply_reduce_fusion = (f32[6,1024]{1,0:T(8,128)S(1)}, bf16[6,1024,128]{2,1,0:T(8,128)(2,1)S(1)}) fusion(f32[6,1024,128]{2,1,0:T(8,128)S(1)} %copy-done.3, bf16[6,1024,1024]{1,2,0:T(8,128)(2,1)S(1)} %fusion.17, bf16[1024,128,1]{1,0,2:T(8,128)(2,1)S(1)} %fusion.69), kind=kOutput, calls=%fused_computation.26 | convolution fusion | flops 1613752320 | bytes 17588224 | tf_op jit(solution)/shard_map/hqk,ke->hqe/dot_general | solution.py:31
  208.1 15.1 %multiply_convert_fusion = bf16[6,1024,1024]{1,2,0:T(8,128)(2,1)} fusion(f32[6,1024]{1,0:T(8,128)S(1)} %get-tuple-element.14, f32[6,1024,1024]{1,2,0:T(8,128)} %get-tuple-element.11, f32[6,1024]{1,0:T(8,128)S(1)} %get-tuple-element.10, bf16[1024,128,1]{1,0,2:T(8,128)(2,1)S(1)} %fusion.69, bf16[6,128,1024]{2,1,0:T(8,128)(2,1)} %get-tuple-element.13), kind=kOutput, calls=%fused_computation.3 | convolution fusion | flops 1635778560 | bytes 39632896 | tf_op jit(solution)/shard_map/hqe,ke->hqk/dot_general | solution.py:34
  223.2 8.4 %fusion.60 = bf16[1024,128]{1,0:T(8,128)(2,1)S(1)} fusion(bf16[6,1024,1024]{1,2,0:T(8,128)(2,1)} %multiply_convert_fusion, bf16[6,128,1024]{2,1,0:T(8,128)(2,1)} %fusion.22), kind=kOutput, calls=%fused_computation.53 | convolution fusion | flops 1610874880 | bytes 14417920 | tf_op jit(solution)/shard_map/hqk,hqe->ke/dot_general | solution.py:38
  231.6 8.2 %fusion.19 = f32[6144,128]{0,1:T(8,128)} fusion(bf16[1024,128]{1,0:T(8,128)(2,1)S(1)} %fusion.60, bf16[1024,6144]{1,0:T(8,128)(2,1)} %all-gather.3.cloned.1.call-done, pred[]{:T(512)S(6)} %eq.5), kind=kOutput, calls=%fused_computation.24 | convolution fusion | flops 1611399168 | bytes 15990785 | tf_op jit(solution)/shard_map/tc,te->ce/dot_general | solution.py:46
  239.8 0.4 reduce-scatter.8.cloned.1.call-start
  240.3 8.4 %fusion.54 = bf16[1024,128]{1,0:T(8,128)(2,1)S(1)} fusion(bf16[6,1024,1024]{1,2,0:T(8,128)(2,1)} %copy-done.2, bf16[6,128,1024]{2,1,0:T(8,128)(2,1)} %get-tuple-element.13), kind=kOutput, calls=%fused_computation.51 | convolution fusion | flops 1610743808 | bytes 14417920 | tf_op jit(solution)/shard_map/hqk,hqe->ke/dot_general | solution.py:39
  248.7 0.7 copy-done.7
  249.4 8.3 %fusion.18 = f32[6144,128]{0,1:T(8,128)} fusion(bf16[1024,128]{1,0:T(8,128)(2,1)S(1)} %fusion.54, bf16[1024,6144]{1,0:T(8,128)(2,1)} %all-gather.3.cloned.1.call-done, pred[]{:T(512)S(6)} %eq.5), kind=kOutput, calls=%fused_computation.22 | convolution fusion | flops 1611399168 | bytes 15990785 | tf_op jit(solution)/shard_map/tc,te->ce/dot_general | solution.py:47
  257.7 10.2 %fusion.35 = f32[1024,6144]{1,0:T(8,128)} fusion(bf16[1024,128]{1,0:T(8,128)(2,1)S(1)} %fusion.60, bf16[6144,1,128]{2,0,1:T(8,128)(2,1)S(1)} %copy-done), kind=kOutput, calls=%fused_computation.40 | convolution fusion | flops 1610612736 | bytes 27000832 | tf_op jit(solution)/shard_map/te,ce->tc/dot_general | solution.py:42
  267.9 10.1 %fusion.28 = f32[1024,6144]{1,0:T(8,128)} fusion(bf16[1024,128]{1,0:T(8,128)(2,1)S(1)} %copy-done.8, bf16[6144,1,128]{2,0,1:T(8,128)(2,1)S(1)} %copy-done.5), kind=kOutput, calls=%fused_computation.32 | convolution fusion | flops 1610612736 | bytes 27000832 | tf_op jit(solution)/shard_map/te,ce->tc/dot_general | solution.py:43
  278.1 8.2 %multiply_convert_fusion.1 = bf16[6,1024,128]{2,1,0:T(8,128)(2,1)S(1)} fusion(bf16[6,1024,1024]{1,2,0:T(8,128)(2,1)} %multiply_convert_fusion, bf16[1024,128,1]{1,0,2:T(8,128)(2,1)S(1)} %copy-done.10), kind=kOutput, calls=%fused_computation.27 | convolution fusion | flops 1612185600 | bytes 14417920 | tf_op jit(solution)/shard_map/hqk,ke->hqe/dot_general | solution.py:37
  286.3 1.1 copy-done.6
  287.4 28.5 %fusion.1 = f32[1024,6144]{1,0:T(8,128)} fusion(f32[1024,6144]{1,0:T(8,128)} %fusion.28, f32[1024,6144]{1,0:T(8,128)} %fusion.35, bf16[6,1024,128]{2,1,0:T(8,128)(2,1)S(1)} %multiply_convert_fusion.1, bf16[6144,6,128]{2,0,1:T(8,128)(2,1)} %param.8), kind=kOutput, calls=%fused_computation.2 | convolution fusion | flops 9676259328 | bytes 86507520 | tf_op jit(solution)/shard_map/hte,che->tc/dot_general | solution.py:41
  316.0 17.2 %fusion.14 = f32[6144,6,128]{0,2,1:T(8,128)} fusion(bf16[6,1024,128]{2,1,0:T(8,128)(2,1)} %copy-done.6, bf16[1024,6144]{1,0:T(8,128)(2,1)} %all-gather.3.cloned.1.call-done), kind=kOutput, calls=%fused_computation.19 | convolution fusion | flops 9663676416 | bytes 33030144 | tf_op jit(solution)/shard_map/tc,hte->che/dot_general | solution.py:40
  333.2 18.6 %copy.21 = f32[6144,6,128]{2,0,1:T(8,128)} copy(f32[6144,6,128]{0,2,1:T(8,128)} %fusion.14) | data formatting | bytes 37748736
  351.8 16.8 %fusion.3 = f32[6,128,6144]{2,1,0:T(8,128)} fusion(bf16[6,1024,128]{2,1,0:T(8,128)(2,1)S(1)} %get-tuple-element.15, bf16[1024,6144]{1,0:T(8,128)(2,1)} %all-gather.5.cloned.1.call-done), kind=kOutput, calls=%fused_computation.7 | convolution fusion | flops 9663676416 | bytes 33030144 | tf_op jit(solution)/shard_map/hte,tc->hec/dot_general | solution.py:33
  368.6 1.9 copy.22
  370.5 1.9 copy.23
  372.4 95.6 %reduce-scatter.4.cloned.1.call-done = f32[128,6144]{1,0:T(8,128)} async-done(((f32[1024,6144]{1,0:T(8,128)}), f32[128,6144]{1,0:T(8,128)}) %reduce-scatter.4.cloned.1.call-update) | async-done | bytes 3145744 | tf_op jit(solution)/shard_map/reduce_scatter | solution.py:44
  468.0 3.2 convert_element_type.51
  (29 shorter events, 0.3 us)
Async XLA Ops:
  7.2 156.3 %copy-start = (bf16[6144,1,128]{2,0,1:T(8,128)(2,1)S(1)}, bf16[6144,1,128]{2,0,1:T(8,128)(2,1)}, u32[]{:S(2)}) copy-start(bf16[6144,1,128]{2,0,1:T(8,128)(2,1)} %param.9) | copy-start | bytes 4718596
  7.2 71.8 %all-gather.5.cloned.1.call-start = ((), (), s32[]{:S(2)}) async-start(), calls=%async_computation.4 | async-start | bytes 14155776 | tf_op jit(solution)/shard_map/all_gather | solution.py:21
  7.9 139.2 %all-gather.3.cloned.1.call-start = ((), (), s32[]{:S(2)}) async-start(), calls=%async_computation.3 | async-start | bytes 14155776 | tf_op jit(solution)/shard_map/all_gather | solution.py:20
  8.7 359.9 %reduce-scatter.6.cloned.1.call-start = ((), (), s32[]{:S(2)}) async-start(), calls=%async_computation.6 | async-start | bytes 3538944 | tf_op jit(solution)/shard_map/reduce_scatter | solution.py:50
  147.1 16.4 %copy-start.1 = (bf16[1024,6144]{1,0:T(8,128)(2,1)S(1)}, bf16[1024,6144]{1,0:T(8,128)(2,1)}, u32[]{:S(2)}) copy-start(bf16[1024,6144]{1,0:T(8,128)(2,1)} %all-gather.3.cloned.1.call-done) | copy-start | bytes 37748740
  166.9 14.6 %copy-start.9 = (bf16[1024,128,1]{1,0,2:T(8,128)(2,1)}, bf16[1024,128,1]{1,0,2:T(8,128)(2,1)S(1)}, u32[]{:S(2)}) copy-start(bf16[1024,128,1]{1,0,2:T(8,128)(2,1)S(1)} %fusion.72) | copy-start | bytes 786436
  181.5 10.3 %copy-start.4 = (bf16[6144,1,128]{2,0,1:T(8,128)(2,1)S(1)}, bf16[6144,1,128]{2,0,1:T(8,128)(2,1)}, u32[]{:S(2)}) copy-start(bf16[6144,1,128]{2,0,1:T(8,128)(2,1)} %param.10) | copy-start | bytes 4718596
  191.7 16.3 %copy-start.2 = (bf16[6,1024,1024]{1,2,0:T(8,128)(2,1)}, bf16[6,1024,1024]{1,2,0:T(8,128)(2,1)S(1)}, u32[]{:S(2)}) copy-start(bf16[6,1024,1024]{1,2,0:T(8,128)(2,1)S(1)} %fusion.17) | copy-start | bytes 37748740
  191.8 11.2 %copy-start.3 = (f32[6,1024,128]{2,1,0:T(8,128)S(1)}, f32[6,1024,128]{2,1,0:T(8,128)}, u32[]{:S(2)}) copy-start(f32[6,1024,128]{2,1,0:T(8,128)} %copy.32) | copy-start | bytes 9437188
  239.8 130.7 %reduce-scatter.8.cloned.1.call-start = ((), (), s32[]{:S(2)}) async-start(), calls=%async_computation.7 | async-start | bytes 3538944 | tf_op jit(solution)/shard_map/reduce_scatter | solution.py:51
  248.7 0.7 copy-start.7
  257.7 10.2 %copy-start.5 = (bf16[6144,1,128]{2,0,1:T(8,128)(2,1)S(1)}, bf16[6144,1,128]{2,0,1:T(8,128)(2,1)}, u32[]{:S(2)}) copy-start(bf16[6144,1,128]{2,0,1:T(8,128)(2,1)} %param.10) | copy-start | bytes 4718596
  257.7 10.2 %copy-start.8 = (bf16[1024,128]{1,0:T(8,128)(2,1)S(1)}, bf16[1024,128]{1,0:T(8,128)(2,1)}, u32[]{:S(2)}) copy-start(bf16[1024,128]{1,0:T(8,128)(2,1)} %copy-done.7) | copy-start | bytes 786436
  267.9 10.1 %copy-start.10 = (bf16[1024,128,1]{1,0,2:T(8,128)(2,1)S(1)}, bf16[1024,128,1]{1,0,2:T(8,128)(2,1)}, u32[]{:S(2)}) copy-start(bf16[1024,128,1]{1,0,2:T(8,128)(2,1)} %copy-done.9) | copy-start | bytes 786436
  278.0 190.0 %reduce-scatter.4.cloned.1.call-start = ((), (), s32[]{:S(2)}) async-start(), calls=%async_computation.5 | async-start | bytes 28311552 | tf_op jit(solution)/shard_map/reduce_scatter | solution.py:44
  286.2 1.1 copy-start.6
Sparse Core Ops, SparseCore 0:
  9.8 69.1 all-gather.4
  80.8 66.2 all-gather.2
  239.9 37.4 reduce-scatter.5
  280.6 37.4 reduce-scatter.7
  321.5 146.4 reduce-scatter.3
where the time goes:
time: 486 us; the launch traced here: 478 us
  waiting for transfers between devices  215 us (44%)
  matrix products  207 us (43%)
  local copies, waits for them, and re-layouts  27.9 us (6%)
  between operations  14.1 us (3%)
  other arithmetic  13.8 us (3%)
    reduce_scatter x1, waiting for transfers between devices, local_grads(): lax.psum_scatter(dx_part, 'tp', scatter_dimension=0, tiled=True)  95.6 us
    all_gather x1, waiting for transfers between devices, local_grads(): dy_full = lax.all_gather(dy_blk, 'tp', axis=0, tiled=True)  69.9 us
    all_gather x1, waiting for transfers between devices, local_grads(): x_full = lax.all_gather(x_blk, 'tp', axis=0, tiled=True)  47.5 us
    dot_general x1, matrix products, local_grads(): jnp.einsum('hte,che->tc', d_query, wq_loc, preferred_element_type=f32)  28.5 us
    unnamed x26, local copies, waits for them, and re-layouts  27.9 us
    dot_general x1, matrix products, local_grads(): jnp.einsum('tc,hte->che', x_full, d_query, preferred_element_type=f32)  17.2 us
    dot_general x1, matrix products, local_grads(): jnp.einsum('tc,hec->hte', dy_full, wo_loc, preferred_element_type=f32)  17.1 us
    dot_general x1, matrix products, local_grads(): jnp.einsum('hte,tc->hec', attn_out, dy_full, preferred_element_type=f32)  16.8 us
  transfers between devices with their start and end apart: 5, of which 3 were waited for; matrix products, arithmetic and copies ran while one was open for 32% of the time, Pallas kernels for 0%

commit v1 on v0

v1 whole, which is shorter than its diff:
```python
import functools

import jax
import jax.numpy as jnp
from jax import lax
from jax.experimental import pallas as pl
from jax.experimental.pallas import tpu as pltpu
from jax.sharding import PartitionSpec as P

MESH = pl.DeviceIdType.MESH
F32 = jnp.float32
BF16 = jnp.bfloat16
ANY = pl.BlockSpec(memory_space=pl.ANY)
VM = pl.BlockSpec(memory_space=pltpu.VMEM)
BLK = 128
HALF = 64
CHUNK = 256
X_NBR, Y_NBR, SIB = 2, 4, 1


def mm(a, b, ca, cb):
    return lax.dot_general(a, b, (((ca,), (cb,)), ((), ())), preferred_element_type=F32)


def rows_of(chunk):
    return pl.ds(pl.multiple_of(chunk * CHUNK, CHUNK), CHUNK)


def attend_chunk(chunk, n_heads, scale, q_ref, do_ref, k_ref, v_ref, put, dk_ref, dv_ref):
    for last in range(q_ref.shape[0] // CHUNK):

        @pl.when(chunk == last)
        def _(last=last):
            span = (last + 1) * CHUNK
            rows = pl.ds(last * CHUNK, CHUNK)

            def head(h, carry):
                cols = pl.ds(pl.multiple_of(h * BLK, BLK), BLK)
                q = q_ref[rows, cols]
                d_out = do_ref[rows, cols]
                keys = k_ref[:span, :]
                vals = v_ref[:span, :]
                s = mm(q, keys, 1, 1) * scale
                row = lax.broadcasted_iota(jnp.int32, (CHUNK, CHUNK), 0)
                col = lax.broadcasted_iota(jnp.int32, (CHUNK, CHUNK), 1)
                s_diag = jnp.where(row >= col, s[:, span - CHUNK :], -jnp.inf)
                s = s_diag if last == 0 else jnp.concatenate([s[:, : span - CHUNK], s_diag], axis=1)
                e = jnp.exp(s - jnp.max(s, axis=1, keepdims=True))
                p = e * (1.0 / jnp.sum(e, axis=1, keepdims=True))
                pb = p.astype(BF16)
                o = mm(pb, vals, 1, 0).astype(BF16)
                delta = jnp.sum(d_out.astype(F32) * o.astype(F32), axis=1, keepdims=True)
                ds = (p * (mm(d_out, vals, 1, 1) - delta)).astype(BF16)
                dq = (mm(ds, keys, 1, 0) * scale).astype(BF16)
                put(h, o, dq)
                dk_ref[:span, :] += mm(ds, q, 0, 0)
                dv_ref[:span, :] += mm(pb, d_out, 0, 0)
                return carry

            lax.fori_loop(0, n_heads, head, 0)


def gather_kernel(
    n_heads, scale,
    x_ref, dy_ref, wq_ref, wk_ref, wv_ref, wo_ref,
    xf_ref, dyf_ref, wqs_ref, q_ref, k_ref, v_ref, do_ref, dqm_ref, dqs_ref, o_ref, dk_ref, dv_ref,
    xb, yb, wq, wkv, wo, dq_tmp, send_sem, recv_sem, wsend, wrecv, lsem, osem,
):
    me = lax.axis_index("tp")
    chip = me // 2
    core = lax.rem(me, 2)
    partner = {m: jnp.bitwise_xor(me, m) for m in range(1, 8)}
    barrier = pltpu.get_barrier_semaphore()
    for m in (SIB, X_NBR, Y_NBR):
        pl.semaphore_signal(barrier, inc=1, device_id={"tp": partner[m]}, device_id_type=MESH)
    pl.semaphore_wait(barrier, 3)

    bufs = (xb, yb)
    srcs = (x_ref, dy_ref)
    outs = (xf_ref, dyf_ref)
    counts = [0, 0]
    sends = []

    def part(t, block, half):
        return bufs[t].at[block, pl.ds(half * HALF, HALF)]

    def send(t, block, half, mask, own=False):
        src = srcs[t].at[pl.ds(half * HALF, HALF)] if own else part(t, block, half)
        copy = pltpu.make_async_remote_copy(
            src_ref=src,
            dst_ref=part(t, block, half),
            send_sem=send_sem.at[t, counts[t]],
            recv_sem=recv_sem.at[t, block, half],
            device_id={"tp": partner[mask]},
            device_id_type=MESH,
        )
        counts[t] += 1
        copy.start()
        sends.append(copy)

    def arrive(t, mask, half):
        block = partner[mask]
        pltpu.make_async_remote_copy(
            src_ref=part(t, block, half),
            dst_ref=part(t, block, half),
            send_sem=send_sem.at[t, 0],
            recv_sem=recv_sem.at[t, block, half],
            device_id={"tp": partner[SIB]},
            device_id_type=MESH,
        ).wait_recv()

    for half in range(2):
        send(0, me, half, X_NBR, own=True)
        send(0, me, half, Y_NBR, own=True)
    send(1, me, 0, X_NBR, own=True)
    send(1, me, 1, Y_NBR, own=True)
    loads = [
        pltpu.make_async_copy(x_ref, xb.at[me], lsem.at[0]),
        pltpu.make_async_copy(wq_ref, wq, lsem.at[1]),
        pltpu.make_async_copy(wk_ref, wkv.at[0], lsem.at[2]),
        pltpu.make_async_copy(wv_ref, wkv.at[1], lsem.at[3]),
        pltpu.make_async_copy(dy_ref, yb.at[me], lsem.at[4]),
        pltpu.make_async_copy(wo_ref, wo, lsem.at[5]),
    ]
    for copy in loads:
        copy.start()
    for half in range(2):
        send(0, me, half, SIB, own=True)
    for half in range(2):
        send(1, me, half, SIB, own=True)
    w_copy = pltpu.make_async_remote_copy(
        src_ref=wq_ref, dst_ref=wqs_ref, send_sem=wsend, recv_sem=wrecv,
        device_id={"tp": partner[SIB]}, device_id_type=MESH,
    )
    w_copy.start()
    dk_ref[...] = jnp.zeros_like(dk_ref)
    dv_ref[...] = jnp.zeros_like(dv_ref)

    writes = []

    def chunk_of(p):
        return jnp.bitwise_xor(chip, p)

    def write_out(t, p):
        chunk = chunk_of(p)
        for i in range(2):
            copy = pltpu.make_async_copy(
                bufs[t].at[2 * chunk + i],
                outs[t].at[pl.ds(pl.multiple_of((2 * chunk + i) * BLK, BLK), BLK)],
                osem.at[t, p, i],
            )
            copy.start()
            writes.append(copy)

    def project(p):
        chunk = chunk_of(p)
        rows = rows_of(chunk)
        x = xb[pl.ds(2 * chunk, 2)].reshape(CHUNK, xb.shape[2])

        def pair(j, carry):
            w = jnp.concatenate([wq[2 * j], wq[2 * j + 1]], axis=1)
            q_ref[rows, pl.ds(pl.multiple_of(j * 2 * BLK, 2 * BLK), 2 * BLK)] = mm(x, w, 1, 0).astype(BF16)
            return carry

        lax.fori_loop(0, n_heads // 2, pair, 0)
        kv = mm(x, jnp.concatenate([wkv[0], wkv[1]], axis=1), 1, 0).astype(BF16)
        k_ref[rows, :] = kv[:, :BLK]
        v_ref[rows, :] = kv[:, BLK:]
        write_out(0, p)

    def project_out(p):
        chunk = chunk_of(p)
        rows = rows_of(chunk)
        y = yb[pl.ds(2 * chunk, 2)].reshape(CHUNK, yb.shape[2])

        def pair(j, carry):
            w = wo[pl.ds(2 * j, 2)].reshape(2 * BLK, wo.shape[2])
            do_ref[rows, pl.ds(pl.multiple_of(j * 2 * BLK, 2 * BLK), 2 * BLK)] = mm(y, w, 1, 1).astype(BF16)
            return carry

        lax.fori_loop(0, n_heads // 2, pair, 0)
        write_out(1, p)

    def both(t, mask):
        arrive(t, mask, 0)
        arrive(t, mask, 1)

    for copy in loads[:4]:
        copy.wait()
    both(0, SIB)
    project(0)
    for copy in loads[4:]:
        copy.wait()
    both(1, SIB)
    project_out(0)
    arrive(0, X_NBR, 0)
    send(0, partner[X_NBR], 0, Y_NBR)
    arrive(0, Y_NBR, 1)
    send(0, partner[Y_NBR], 1, X_NBR)
    send(0, partner[X_NBR], 0, SIB)
    send(0, partner[Y_NBR], 1, SIB)
    arrive(0, X_NBR, 1)
    send(0, partner[X_NBR], 1, SIB)
    arrive(0, Y_NBR, 0)
    send(0, partner[Y_NBR], 0, SIB)
    both(0, X_NBR ^ SIB)
    project(1)
    both(0, Y_NBR ^ SIB)
    project(2)
    arrive(1, X_NBR, 0)
    send(1, partner[X_NBR], 0, Y_NBR)
    arrive(1, Y_NBR, 1)
    send(1, partner[Y_NBR], 1, X_NBR)
    send(1, me, 1, X_NBR, own=True)
    send(1, me, 0, Y_NBR, own=True)
    send(1, partner[X_NBR], 0, SIB)
    send(1, partner[Y_NBR], 1, SIB)
    diag = X_NBR ^ Y_NBR
    for t in range(2):
        for half in range(2):
            arrive(t, diag, half)
            send(t, partner[diag], half, SIB)
        both(t, diag ^ SIB)
        if t == 0:
            project(3)
        else:
            project_out(3)

    chunk_d = chunk_of(3)

    def put(h, o, dq):
        cols = pl.ds(pl.multiple_of(h * BLK, BLK), BLK)
        o_ref[:, cols] = o
        dq_tmp[0, :, cols] = dq[:BLK]
        dq_tmp[1, :, cols] = dq[BLK:]

    attend_chunk(chunk_d, n_heads, scale, q_ref, do_ref, k_ref, v_ref, put, dk_ref, dv_ref)
    dqm_ref[...] = dq_tmp[core]
    dqs_ref[...] = dq_tmp[1 - core]
    arrive(1, X_NBR, 1)
    send(1, partner[X_NBR], 1, SIB)
    arrive(1, Y_NBR, 0)
    send(1, partner[Y_NBR], 0, SIB)
    both(1, X_NBR ^ SIB)
    project_out(1)
    both(1, Y_NBR ^ SIB)
    project_out(2)
    for copy in sends:
        copy.wait_send()
    w_copy.wait()
    for copy in writes:
        copy.wait()


def gather_project(x_blk, dy_blk, wq, wk, wv, wo, n_dev, scale):
    n_heads, dim, hd = wq.shape
    tokens = x_blk.shape[0] * n_dev
    wide = n_heads * hd
    sds = jax.ShapeDtypeStruct
    return pl.pallas_call(
        functools.partial(gather_kernel, n_heads, scale),
        out_shape=(
            sds((tokens, dim), BF16), sds((tokens, dim), BF16), sds(wq.shape, BF16),
            sds((tokens, wide), BF16), sds((tokens, hd), BF16), sds((tokens, hd), BF16), sds((tokens, wide), BF16),
            sds((BLK, wide), BF16), sds((BLK, wide), BF16), sds((CHUNK, wide), BF16),
            sds((tokens, hd), F32), sds((tokens, hd), F32),
        ),
        in_specs=[ANY] * 6,
        out_specs=(ANY,) * 3 + (VM,) * 9,
        scratch_shapes=[
            pltpu.VMEM((n_dev, BLK, dim), BF16),
            pltpu.VMEM((n_dev, BLK, dim), BF16),
            pltpu.VMEM(wq.shape, BF16),
            pltpu.VMEM((2, dim, hd), BF16),
            pltpu.VMEM(wo.shape, BF16),
            pltpu.VMEM((2, BLK, wide), BF16),
            pltpu.SemaphoreType.DMA((2, 14)),
            pltpu.SemaphoreType.DMA((2, n_dev, 2)),
            pltpu.SemaphoreType.DMA,
            pltpu.SemaphoreType.DMA,
            pltpu.SemaphoreType.DMA((6,)),
            pltpu.SemaphoreType.DMA((2, 4, 2)),
        ],
        compiler_params=pltpu.CompilerParams(
            collective_id=0, has_side_effects=True, vmem_limit_bytes=67043328
        ),
        name="gather_project",
    )(x_blk, dy_blk, wq, wk, wv, wo)


def attend_kernel(
    n_heads, scale,
    q_ref, k_ref, v_ref, do_ref, od_ref, dqd_ref, dqs_ref, dk0_ref, dv0_ref,
    o_ref, dq_ref, mine_ref, give_ref, dk_ref, dv_ref,
):
    me = lax.axis_index("tp")
    chip = me // 2
    core = lax.rem(me, 2)
    wide = q_ref.shape[1]
    dk_ref[...] = dk0_ref[...]
    dv_ref[...] = dv0_ref[...]

    def step(i, carry):
        chunk = jnp.bitwise_xor(chip, lax.rem(i + 1, 3))
        rows = rows_of(chunk)

        def put(h, o, dq):
            cols = pl.ds(pl.multiple_of(h * BLK, BLK), BLK)
            o_ref[rows, cols] = o
            dq_ref[rows, cols] = dq

        attend_chunk(chunk, n_heads, scale, q_ref, do_ref, k_ref, v_ref, put, dk_ref, dv_ref)
        return carry

    lax.fori_loop(0, 3, step, 0)
    chunk_d = jnp.bitwise_xor(chip, 3)
    o_ref[rows_of(chunk_d), :] = od_ref[...]
    dq_ref[pl.ds(pl.multiple_of(chunk_d * CHUNK + core * BLK, BLK), BLK), :] = dqd_ref[...]
    dq_ref[pl.ds(pl.multiple_of(chunk_d * CHUNK + (1 - core) * BLK, BLK), BLK), :] = dqs_ref[...]
    for p in range(4):
        chunk = jnp.bitwise_xor(chip, p)
        for ref, cls in ((mine_ref, core), (give_ref, 1 - core)):
            rows = pl.ds(pl.multiple_of(chunk * CHUNK + cls * BLK, BLK), BLK)
            ref[p, :, :wide] = dq_ref[rows, :]
            ref[p, :, wide : wide + BLK] = (dk_ref[rows, :] * scale).astype(BF16)
            ref[p, :, wide + BLK :] = dv_ref[rows, :].astype(BF16)


def attend(q, k, v, d_out, o_d, dqm_d, dqs_d, dk0, dv0, n_heads, scale):
    tokens, wide = q.shape
    hd = k.shape[1]
    sds = jax.ShapeDtypeStruct
    pairs = tokens * tokens * n_heads // 2
    return pl.pallas_call(
        functools.partial(attend_kernel, n_heads, scale),
        out_shape=(
            sds((tokens, wide), BF16), sds((tokens, wide), BF16),
            sds((4, BLK, wide + 2 * hd), BF16), sds((4, BLK, wide + 2 * hd), BF16),
        ),
        in_specs=[VM] * 9,
        out_specs=(VM,) * 4,
        scratch_shapes=[pltpu.VMEM((tokens, hd), F32), pltpu.VMEM((tokens, hd), F32)],
        compiler_params=pltpu.CompilerParams(vmem_limit_bytes=48 * 2**20),
        cost_estimate=pl.CostEstimate(flops=pairs * hd * 24, bytes_accessed=12 * 2**20, transcendentals=pairs),
        name="attend",
    )(q, k, v, d_out, o_d, dqm_d, dqs_d, dk0, dv0)


def dx_kernel(groups, wide, mine_ref, got_ref, wa_ref, wb_ref, sa_ref, sb_ref, *out_refs):
    lhs = jnp.concatenate(
        [
            jnp.concatenate([mine_ref[g, :, :wide] for g in groups], axis=0),
            jnp.concatenate([got_ref[g, :, :wide] for g in groups], axis=0),
        ],
        axis=1,
    )
    for side, (w_ref, s_ref) in enumerate(((wa_ref, sa_ref), (wb_ref, sb_ref))):
        n = w_ref.shape[0]
        rhs = jnp.concatenate([w_ref[h] for h in range(n)] + [s_ref[h] for h in range(n)], axis=1)
        res = mm(lhs, rhs, 1, 1)
        for i in range(len(groups)):
            out_refs[2 * i + side][...] = res[i * BLK : (i + 1) * BLK]


def dx_partial(mine, got, wq, wqs, groups):
    n_heads, dim, hd = wq.shape
    tile = 512
    half = dim // 2
    steps = half // tile
    rows = BLK * len(groups)
    w_lo = pl.BlockSpec((n_heads, tile, hd), lambda j: (0, j, 0))
    w_hi = pl.BlockSpec((n_heads, tile, hd), lambda j: (0, j + steps, 0))
    whole = pl.BlockSpec(mine.shape, lambda j: (0, 0, 0))
    return pl.pallas_call(
        functools.partial(dx_kernel, groups, n_heads * hd),
        grid=(steps,),
        out_shape=(jax.ShapeDtypeStruct((BLK, half), F32),) * (2 * len(groups)),
        in_specs=[whole, whole, w_lo, w_hi, w_lo, w_hi],
        out_specs=(pl.BlockSpec((BLK, tile), lambda j: (0, j)),) * (2 * len(groups)),
        compiler_params=pltpu.CompilerParams(vmem_limit_bytes=40 * 2**20),
        cost_estimate=pl.CostEstimate(
            flops=4 * rows * dim * n_heads * hd, bytes_accessed=4 * dim * n_heads * hd + 4 * rows * dim, transcendentals=0
        ),
        name="dx_partial",
    )(mine, got, wq, wq, wqs, wqs)


def dwo_kernel(o_ref, dy_ref, out_ref, o_t):
    @pl.when(pl.program_id(0) == 0)
    def _():
        o_t[...] = o_ref[...].T

    res = mm(o_t[...], dy_ref[...], 1, 0)
    for h in range(out_ref.shape[0]):
        out_ref[h] = res[h * BLK : (h + 1) * BLK]


def grad_wo(o, dy_full):
    tokens, wide = o.shape
    dim = dy_full.shape[1]
    tile = 512
    n_heads = wide // BLK
    return pl.pallas_call(
        dwo_kernel,
        grid=(dim // tile,),
        out_shape=jax.ShapeDtypeStruct((n_heads, BLK, dim), F32),
        in_specs=[pl.BlockSpec((tokens, wide), lambda j: (0, 0)), pl.BlockSpec((tokens, tile), lambda j: (0, j))],
        out_specs=pl.BlockSpec((n_heads, BLK, tile), lambda j: (0, 0, j)),
        scratch_shapes=[pltpu.VMEM((wide, tokens), BF16)],
        compiler_params=pltpu.CompilerParams(vmem_limit_bytes=40 * 2**20),
        cost_estimate=pl.CostEstimate(
            flops=2 * tokens * wide * dim, bytes_accessed=2 * tokens * dim + 4 * wide * dim, transcendentals=0
        ),
        name="grad_wo",
    )(o, dy_full)


def dwq_kernel(x_ref, dq_ref, out_ref):
    res = mm(x_ref[...], dq_ref[...], 0, 0)
    for h in range(out_ref.shape[0]):
        out_ref[h] = res[:, h * BLK : (h + 1) * BLK]


def grad_wq(x_full, dq):
    tokens, wide = dq.shape
    dim = x_full.shape[1]
    tile = 512
    n_heads = wide // BLK
    return pl.pallas_call(
        dwq_kernel,
        grid=(dim // tile,),
        out_shape=jax.ShapeDtypeStruct((n_heads, dim, BLK), F32),
        in_specs=[pl.BlockSpec((tokens, tile), lambda j: (0, j)), pl.BlockSpec((tokens, wide), lambda j: (0, 0))],
        out_specs=pl.BlockSpec((n_heads, tile, BLK), lambda j: (0, j, 0)),
        compiler_params=pltpu.CompilerParams(vmem_limit_bytes=40 * 2**20),
        cost_estimate=pl.CostEstimate(
            flops=2 * tokens * wide * dim, bytes_accessed=2 * tokens * dim + 4 * wide * dim, transcendentals=0
        ),
        name="grad_wq",
    )(x_full, dq)


def split3(a):
    hi = a.astype(BF16)
    rest = a - hi.astype(F32)
    mid = rest.astype(BF16)
    low = (rest - mid.astype(F32)).astype(BF16)
    return hi, mid, low


def kv_kernel(me_ref, mine_ref, other_ref, x_ref, dwk_ref, dwv_ref, rows_ref):
    me = me_ref[0]
    chip = me // 2
    core = lax.rem(me, 2)
    wide = mine_ref.shape[2]
    for p in range(4):
        chunk = jnp.bitwise_xor(chip, p)
        for ref, cls in ((mine_ref, core), (other_ref, 1 - core)):
            rows = pl.ds(pl.multiple_of(chunk * CHUNK + cls * BLK, BLK), BLK)
            for i, piece in enumerate(split3(ref[p])):
                rows_ref[rows, i * wide : (i + 1) * wide] = piece
    res = mm(x_ref[...], rows_ref[...], 0, 0)
    res = res[:, :wide] + res[:, wide : 2 * wide] + res[:, 2 * wide :]
    dwk_ref[...] = res[:, :BLK]
    dwv_ref[...] = res[:, BLK:]


def grad_kv(me, mine, other, x_full, n_dev):
    tokens, dim = x_full.shape
    own = dim // n_dev
    whole = pl.BlockSpec(mine.shape, lambda i, m: (0, 0, 0))
    out = pl.BlockSpec((own, BLK), lambda i, m: (0, 0))
    return pl.pallas_call(
        kv_kernel,
        grid_spec=pltpu.PrefetchScalarGridSpec(
            num_scalar_prefetch=1,
            grid=(1,),
            in_specs=[whole, whole, pl.BlockSpec((tokens, own), lambda i, m: (0, m[0]))],
            out_specs=(out, out),
            scratch_shapes=[pltpu.VMEM((tokens, 3 * mine.shape[2]), BF16)],
        ),
        out_shape=(jax.ShapeDtypeStruct((own, BLK), F32),) * 2,
        compiler_params=pltpu.CompilerParams(vmem_limit_bytes=40 * 2**20),
        cost_estimate=pl.CostEstimate(
            flops=2 * tokens * own * 3 * mine.shape[2], bytes_accessed=4 * tokens * own, transcendentals=0
        ),
        name="grad_kv",
    )(me, mine, other, x_full)


def kvdx_kernel(sum_ref, wka_ref, wkb_ref, wva_ref, wvb_ref, pa_ref, pb_ref, oa_ref, ob_ref):
    pieces = split3(sum_ref[0])
    for wk_ref, wv_ref, p_ref, o_ref in (
        (wka_ref, wva_ref, pa_ref, oa_ref),
        (wkb_ref, wvb_ref, pb_ref, ob_ref),
    ):
        w = jnp.concatenate([wk_ref[...], wv_ref[...]], axis=1)
        res = mm(jnp.concatenate(pieces, axis=0), w, 1, 1)
        o_ref[...] = p_ref[...] + (res[:BLK] + res[BLK : 2 * BLK] + res[2 * BLK :])


def kv_dx(total, wk, wv, pa, pb):
    dim, hd = wk.shape
    half = dim // 2
    tile = 1024
    steps = half // tile
    w_lo = pl.BlockSpec((tile, hd), lambda j: (j, 0))
    w_hi = pl.BlockSpec((tile, hd), lambda j: (j + steps, 0))
    col = pl.BlockSpec((BLK, tile), lambda j: (0, j))
    return pl.pallas_call(
        kvdx_kernel,
        grid=(steps,),
        out_shape=(jax.ShapeDtypeStruct((BLK, half), F32),) * 2,
        in_specs=[pl.BlockSpec((1,) + total.shape[1:], lambda j: (0, 0, 0)), w_lo, w_hi, w_lo, w_hi, col, col],
        out_specs=(col, col),
        compiler_params=pltpu.CompilerParams(vmem_limit_bytes=40 * 2**20),
        cost_estimate=pl.CostEstimate(flops=12 * BLK * dim * hd, bytes_accessed=10 * 2**20, transcendentals=0),
        name="kv_dx",
    )(total, wk, wk, wv, wv, pa, pb)


def solution(mesh):
    n_dev = mesh.shape["tp"]

    def swap(a, mask):
        return lax.ppermute(a, "tp", [(i, i ^ mask) for i in range(n_dev)])

    def local_grads(x_blk, dy_blk, wq_loc, w_k, w_v, wo_loc):
        n_heads, hd = wq_loc.shape[1:]
        scale = hd ** -0.5
        wide = n_heads * hd
        wq = jnp.transpose(wq_loc, (1, 0, 2))
        wk = w_k[:, 0, :]
        wv = w_v[:, 0, :]
        me = lax.axis_index("tp").astype(jnp.int32).reshape(1)
        xf, dyf, wqs, q, k, v, d_out, dqm_d, dqs_d, o_d, dk0, dv0 = gather_project(
            x_blk, dy_blk, wq, wk, wv, wo_loc, n_dev, scale
        )
        dqg_d = swap(dqs_d, SIB)
        pd_a, pd_b = dx_partial(dqm_d[None], dqg_d[None], wq, wqs, (0,))
        ra = swap(pd_a, X_NBR)
        rb = swap(pd_b, Y_NBR)
        o, dq, mine, give = attend(q, k, v, d_out, o_d, dqm_d, dqs_d, dk0, dv0, n_heads, scale)
        got = swap(give, SIB)
        kvs = mine[:, :, wide:].astype(F32) + got[:, :, wide:].astype(F32)
        kv_x = swap(kvs, X_NBR)
        kv_y = swap(kvs, Y_NBR)
        px_a, px_b, py_a, py_b, po_a, po_b = dx_partial(mine, got, wq, wqs, (1, 2, 0))
        a2 = swap(px_a, X_NBR)
        b2 = swap(py_b, Y_NBR)
        kv_d = jnp.concatenate([swap(kv_x[:2], Y_NBR), swap(kv_y[2:], X_NBR)], axis=0)
        dwo = grad_wo(o, dyf)
        a3 = swap(py_a + ra, Y_NBR)
        b3 = swap(px_b + rb, X_NBR)
        total = jnp.stack([kvs[p] + kv_x[p ^ 1] + kv_y[p ^ 2] + kv_d[p ^ 3] for p in range(4)])
        other = swap(total, SIB)
        dwq = grad_wq(xf, dq)
        base_a, base_b = kv_dx(total, wk, wv, po_a, po_b)
        dwk, dwv = grad_kv(me, total, other, xf, n_dev)
        dx = jnp.concatenate([(base_a + a2) + a3, (base_b + b2) + b3], axis=1).astype(BF16)
        return dx, jnp.transpose(dwq, (1, 0, 2)), dwo, dwk, dwv

    tok_spec = P(("dp", "tp"))
    return jax.shard_map(
        local_grads,
        mesh=mesh,
        in_specs=(tok_spec, tok_spec, P(None, "tp", None), P(), P(), P("tp")),
        out_specs=(tok_spec, P("dp", "tp", None), tok_spec, tok_spec, tok_spec),
        check_vma=False,
    )
```

time: 486 us -> 290 us (0.60); the launches traced: 478 us -> 289 us
  matrix products: 207 us -> 0 us
  Pallas kernels: 0 us -> 199 us
  waiting for transfers between devices: 215 us -> 42.2 us
  between operations: 14.1 us -> 0.77 us
  starting transfers between devices: 0.6 us -> 13.3 us
    pallas_call x0 -> x8, Pallas kernels: none -> 199 us  [the longest x1 117 us: gather_project(): pl.pallas_call(functools.partial(gather_kernel, n_heads, scale), out_shap...]
    dot_general x16 -> x0, matrix products: 193 us -> none  [the longest x1 28.5 us: local_grads(): jnp.einsum('hte,che->tc', d_query, wq_loc, preferred_element_type=f32)]
    all_gather x2 -> x0, waiting for transfers between devices: 117 us -> none  [the longest x1 69.9 us: local_grads(): dy_full = lax.all_gather(dy_blk, 'tp', axis=0, tiled=True)]
    reduce_scatter x3 -> x0, waiting for transfers between devices: 95.6 us -> none  [the longest x1 95.6 us: local_grads(): lax.psum_scatter(dx_part, 'tp', scatter_dimension=0, tiled=True)]
    ppermute x0 -> x13, waiting for transfers between devices: none -> 42.2 us  [swap(): return lax.ppermute(a, 'tp', [(i, i ^ mask) for i in range(n_dev)])]
    sub x1 -> x0, matrix products: 14.6 us -> none  [local_grads(): attn_prob = jax.nn.softmax(scores, axis=-1)]
    convert_element_type x2 -> x0, other arithmetic: 13.5 us -> none  [the longest x1 10.2 us: local_grads(): prob_bf = attn_prob.astype(bf16)]
    ppermute x0 -> x13, starting transfers between devices: none -> 13.3 us  [swap(): return lax.ppermute(a, 'tp', [(i, i ^ mask) for i in range(n_dev)])]
  transfers between devices with their start and end apart: 5 -> 13, of which waited for: 3 -> 3; matrix products, arithmetic and copies ran while one was open for 32% -> 2% of each run, Pallas kernels for 0% -> 28%
where the time goes in v1:
time: 290 us; the launch traced here: 289 us
  Pallas kernels  199 us (69%)
  waiting for transfers between devices  42.2 us (15%)
  local copies, waits for them, and re-layouts  24.2 us (8%)
  starting transfers between devices  13.3 us (5%)
  other arithmetic  9.3 us (3%)
    pallas_call x1, Pallas kernels, gather_project(): pl.pallas_call(functools.partial(gather_kernel, n_heads, scale), out_shap...  117 us
    ppermute x13, waiting for transfers between devices, swap(): return lax.ppermute(a, 'tp', [(i, i ^ mask) for i in range(n_dev)])  42.2 us
    unnamed x44, local copies, waits for them, and re-layouts  24.2 us
    pallas_call x2, Pallas kernels, dx_partial(): pl.pallas_call(functools.partial(dx_kernel, groups, n_heads * hd), grid=(...  22.8 us
    pallas_call x1, Pallas kernels, attend(): pl.pallas_call(functools.partial(attend_kernel, n_heads, scale), out_shap...  22.6 us
    pallas_call x1, Pallas kernels, grad_wo(): pl.pallas_call(dwo_kernel, grid=(dim // tile,), out_shape=jax.ShapeDtypeS...  14.8 us
    pallas_call x1, Pallas kernels, grad_wq(): pl.pallas_call(dwq_kernel, grid=(dim // tile,), out_shape=jax.ShapeDtypeS...  14.6 us
    ppermute x13, starting transfers between devices, swap(): return lax.ppermute(a, 'tp', [(i, i ^ mask) for i in range(n_dev)])  13.3 us
  transfers between devices with their start and end apart: 13, of which 3 were waited for; matrix products, arithmetic and copies ran while one was open for 2% of the time, Pallas kernels for 28%

profile of v1, /device:TPU:0, one launch (start us, length us, event | category | flops | bytes accessed | tf_op | source)
XLA Modules:
  0.0 288.8 jit_solution(16898156928346789852)
XLA Ops:
  0.6 117.3 %gather_project.1 = (bf16[1024,6144]{1,0:T(8,128)(2,1)}, bf16[1024,6144]{1,0:T(8,128)(2,1)}, bf16[6,6144,128]{2,1,0:T(8,128)(2,1)}, bf16[1024,768]{1,0:T(8,128)(...) custom-call(bf16[128,6144]{1,0:T(8,128)(2,1)} %x_ref.1, ...), custom_call_target="tpu_custom_call" | custom-call | tf_op jit(solution)/shard_map/gather_project/pallas_call | solution.py:260
  117.9 1.3 collective-permute-start.6
  119.2 1.1 copy-done.8
  120.3 1.3 copy-done.10
  121.6 1.0 copy-done.11
  122.7 1.0 copy-done.12
  123.6 0.9 copy-done.13
  126.5 22.6 %attend.1 = (bf16[1024,768]{1,0:T(8,128)(2,1)S(1)}, bf16[1024,768]{1,0:T(8,128)(2,1)}, bf16[4,128,1024]{2,1,0:T(8,128)(2,1)S(1)}, bf16[4,128,1024]{2,1,0:T(8,128)(2,1)S(1)}) custom-call(bf16[1024,768]{1,0:T(8,128)(2,1)} %get-tuple-element.33.q_ref, bf16[1024,128]{1,0:T(8,128)(2,1)S(1)} %copy-done.13, bf16[1024,128]{1,0:T(8,128)(2,1)S(1)} %copy-done.14, ...), custom_call_target="tpu_custom_call" | custom-call | flops 9663676416 | bytes 12582912 | tf_op jit(solution)/shard_map/attend/pallas_call | solution.py:334
  149.1 10.4 %dx_partial.3 = (f32[128,3072]{1,0:T(8,128)S(1)}, f32[128,3072]{1,0:T(8,128)}) custom-call(bf16[1,128,768]{2,1,0:T(8,128)(2,1)S(1)} %bitcast.20, bf16[1,128,768]{2,1,0:T(8,128)(2,1)S(1)} %bitcast.21, bf16[6,6144,128]{2,1,0:T(8,128)(2,1)S(1)} %bitcast.12, bf16[6,6144,128]{2,1,0:T(8,128)(2,1)S(1)} %bitcast.13, ...), custom_call_target="tpu_custom_call" | custom-call | flops 2415919104 | bytes 22020096 | tf_op jit(solution)/shard_map/dx_partial/pallas_call | solution.py:374
  159.5 1.1 collective-permute-start.7
  160.6 3.8 %collective-permute-start.10 = (f32[128,3072]{1,0:T(8,128)}, f32[128,3072]{1,0:T(8,128)S(1)}, u32[]{:S(2)}, u32[]{:S(2)}) collective-permute-start(f32[128,3072]{1,0:T(8,128)} %get-tuple-element.54), channel_id=1, source_target_pairs={{0,4},{1,5},{2,6},{3,7},{4,0},{5,1},{6,2},{7,3}} | collective-permute-start | bytes 4718600 | tf_op jit(solution)/shard_map/ppermute | solution.py:526
  164.7 12.5 %dx_partial.2 = (f32[128,3072]{1,0:T(8,128)}, f32[128,3072]{1,0:T(8,128)S(1)}, f32[128,3072]{1,0:T(8,128)S(1)}, f32[128,3072]{1,0:T(8,128)}, f32[128,3072]{1,0:T(8,128)S(1)}, /*index=5*/f32[128,3072]{1,0:T(8,128)S(1)}) custom-call(bf16[4,128,1024]{2,1,0:T(8,128)(2,1)S(1)} %get-tuple-element.42.mine_ref, ...), custom_call_target="tpu_custom_call" | custom-call | flops 7247757312 | bytes 28311552 | tf_op jit(solution)/shard_map/dx_partial/pallas_call | solution.py:374
  177.2 2.0 collective-permute-start.5
  179.2 30.9 %collective-permute-done.2 = f32[4,128,256]{2,1,0:T(8,128)S(1)} collective-permute-done((f32[4,128,256]{2,1,0:T(8,128)S(1)}, f32[4,128,256]{2,1,0:T(8,128)S(1)}, u32[]{:S(2)}, u32[]{:S(2)}) %collective-permute-start.2) | collective-permute-done | bytes 524320 | tf_op jit(solution)/shard_map/ppermute | solution.py:526
  210.5 1.8 collective-permute-start.4
  212.2 1.3 add.83
  214.2 4.6 %copy-done.2 = bf16[1024,6144]{1,0:T(8,128)(2,1)S(1)} copy-done((bf16[1024,6144]{1,0:T(8,128)(2,1)S(1)}, bf16[1024,6144]{1,0:T(8,128)(2,1)}, u32[]{:S(2)}) %copy-start.2) | copy-done | bytes 12582936
  218.8 14.6 %grad_wq.1 = f32[6,6144,128]{2,1,0:T(8,128)} custom-call(bf16[1024,6144]{1,0:T(8,128)(2,1)S(1)} %copy-done.2, bf16[1024,768]{1,0:T(8,128)(2,1)S(1)} %copy-done.18), custom_call_target="tpu_custom_call" | custom-call | flops 9663676416 | bytes 31457280 | tf_op jit(solution)/shard_map/grad_wq/pallas_call | solution.py:429
  233.4 1.4 collective-permute-start.9
  234.8 1.3 add.86
  236.2 10.3 %collective-permute-done.3 = f32[2,128,256]{2,1,0:T(8,128)S(1)} collective-permute-done((f32[2,128,256]{2,1,0:T(8,128)S(1)}, f32[2,128,256]{2,1,0:T(8,128)S(1)}, u32[]{:S(2)}, u32[]{:S(2)}) %collective-permute-start.3) | collective-permute-done | bytes 262176 | tf_op jit(solution)/shard_map/ppermute | solution.py:526
  246.5 1.1 collective-permute-start.11
  248.6 4.6 %copy-done.9 = bf16[1024,6144]{1,0:T(8,128)(2,1)S(1)} copy-done((bf16[1024,6144]{1,0:T(8,128)(2,1)S(1)}, bf16[1024,6144]{1,0:T(8,128)(2,1)}, u32[]{:S(2)}) %copy-start.9) | copy-done | bytes 12582936
  253.2 14.8 %grad_wo.1 = f32[6,128,6144]{2,1,0:T(8,128)} custom-call(bf16[1024,768]{1,0:T(8,128)(2,1)S(1)} %copy-done.17, bf16[1024,6144]{1,0:T(8,128)(2,1)S(1)} %copy-done.9), custom_call_target="tpu_custom_call" | custom-call | flops 9663676416 | bytes 31457280 | tf_op jit(solution)/shard_map/grad_wo/pallas_call | solution.py:403
  268.0 1.4 copy-done.5
  269.4 1.4 copy-done.7
  270.8 3.1 %kv_dx.1 = (f32[128,3072]{1,0:T(8,128)S(1)}, f32[128,3072]{1,0:T(8,128)S(1)}) custom-call(f32[4,128,256]{2,1,0:T(8,128)} %pad_maximum_fusion.1.sum_ref.mine_ref, bf16[6144,128]{1,0:T(8,128)(2,1)S(1)} %bitcast.15, bf16[6144,128]{1,0:T(8,128)(2,1)S(1)} %bitcast.16, bf16[6144,128]{1,0:T(8,128)(2,1)S(1)} %bitcast.18, bf16[6144,128]{1,0:T(8,128)(2,1)S(1)} %bitcast.19, ...), custom_call_target="tpu_custom_call" | custom-call | flops 1207959552 | bytes 10485760 | tf_op jit(solution)/shard_map/kv_dx/pallas_call | solution.py:510
  274.0 4.6 %copy-done.3 = bf16[1024,6144]{1,0:T(8,128)(2,1)S(1)} copy-done((bf16[1024,6144]{1,0:T(8,128)(2,1)S(1)}, bf16[1024,6144]{1,0:T(8,128)(2,1)}, u32[]{:S(2)}) %copy-start.3) | copy-done | bytes 12582936
  278.5 3.8 %grad_kv.1 = (f32[768,128]{1,0:T(8,128)}, f32[768,128]{1,0:T(8,128)}) custom-call(s32[1]{0:T(128)} %bitcast.6.me_ref, f32[4,128,256]{2,1,0:T(8,128)} %pad_maximum_fusion.1.sum_ref.mine_ref, f32[4,128,256]{2,1,0:T(8,128)} %collective-permute-done.12.other_ref, bf16[1024,6144]{1,0:T(8,128)(2,1)S(1)} %copy-done.3), custom_call_target="tpu_custom_call" | custom-call | flops 1207959552 | bytes 3145728 | tf_op jit(solution)/shard_map/grad_kv/pallas_call | solution.py:473
  282.4 2.1 add_convert_fusion.1
  285.4 2.1 add_convert_fusion
  287.6 1.3 pad_maximum_fusion
  (57 shorter events, 5.1 us)
Async XLA Ops:
  117.9 31.2 %collective-permute-start.6 = (bf16[128,768]{1,0:T(8,128)(2,1)}, bf16[128,768]{1,0:T(8,128)(2,1)S(1)}, u32[]{:S(2)}, u32[]{:S(2)}) collective-permute-start(bf16[128,768]{1,0:T(8,128)(2,1)} %get-tuple-element.39.dqs_ref), channel_id=1, source_target_pairs={{0,1},{1,0},{2,3},{3,2},{4,5},{5,4},{6,7},{7,6}} | collective-permute-start | bytes 589832 | tf_op jit(solution)/shard_map/ppermute | solution.py:526
  119.2 29.9 %slice-start = ((s8[9437184]{0:T(1024)(128)(4,1)}), s8[4194304]{0:T(1024)(128)(4,1)S(1)}, s32[]{:S(2)}) async-start(s8[9437184]{0:T(1024)(128)(4,1)} %bitcast.10), calls=%async_computation | async-start | bytes 8388608
  119.2 1.1 copy-start.8
  120.3 1.3 copy-start.10
  121.6 1.0 copy-start.11
  122.7 1.0 copy-start.12
  126.5 22.6 %slice-start.1 = ((s8[9437184]{0:T(1024)(128)(4,1)}), s8[4194304]{0:T(1024)(128)(4,1)S(1)}, s32[]{:S(2)}) async-start(s8[9437184]{0:T(1024)(128)(4,1)} %bitcast.10), calls=%async_computation.1 | async-start | bytes 8388608
  126.5 22.6 %slice-start.2 = ((s8[9437184]{0:T(1024)(128)(4,1)}), s8[1048576]{0:T(1024)(128)(4,1)S(1)}, s32[]{:S(2)}) async-start(s8[9437184]{0:T(1024)(128)(4,1)} %bitcast.10), calls=%async_computation.2 | async-start | bytes 2097152
  149.1 10.4 %copy-start.16 = (bf16[1024,768]{1,0:T(8,128)(2,1)}, bf16[1024,768]{1,0:T(8,128)(2,1)S(1)}, u32[]{:S(2)}) copy-start(bf16[1024,768]{1,0:T(8,128)(2,1)S(1)} %get-tuple-element.57.o_ref) | copy-start | bytes 4718596
  149.1 15.4 %collective-permute-start = (bf16[4,128,1024]{2,1,0:T(8,128)(2,1)S(1)}, bf16[4,128,1024]{2,1,0:T(8,128)(2,1)S(1)}, u32[]{:S(2)}, u32[]{:S(2)}) collective-permute-start(bf16[4,128,1024]{2,1,0:T(8,128)(2,1)S(1)} %get-tuple-element.43), channel_id=1, source_target_pairs={{0,1},{1,0},{2,3},{3,2},{4,5},{5,4},{6,7},{7,6}} | collective-permute-start | bytes 3145736 | tf_op jit(solution)/shard_map/ppermute | solution.py:526
  159.5 52.7 %collective-permute-start.7 = (f32[128,3072]{1,0:T(8,128)S(1)}, f32[128,3072]{1,0:T(8,128)S(1)}, u32[]{:S(2)}, u32[]{:S(2)}) collective-permute-start(f32[128,3072]{1,0:T(8,128)S(1)} %get-tuple-element.50), channel_id=1, source_target_pairs={{0,2},{1,3},{2,0},{3,1},{4,6},{5,7},{6,4},{7,5}} | collective-permute-start | bytes 4718600 | tf_op jit(solution)/shard_map/ppermute | solution.py:526
  160.6 72.8 %collective-permute-start.10 = (f32[128,3072]{1,0:T(8,128)}, f32[128,3072]{1,0:T(8,128)S(1)}, u32[]{:S(2)}, u32[]{:S(2)}) collective-permute-start(f32[128,3072]{1,0:T(8,128)} %get-tuple-element.54), channel_id=1, source_target_pairs={{0,4},{1,5},{2,6},{3,7},{4,0},{5,1},{6,2},{7,3}} | collective-permute-start | bytes 4718600 | tf_op jit(solution)/shard_map/ppermute | solution.py:526
  164.6 45.5 %collective-permute-start.2 = (f32[4,128,256]{2,1,0:T(8,128)S(1)}, f32[4,128,256]{2,1,0:T(8,128)S(1)}, u32[]{:S(2)}, u32[]{:S(2)}) collective-permute-start(f32[4,128,256]{2,1,0:T(8,128)S(1)} %convert_add_fusion), channel_id=1, source_target_pairs={{0,4},{1,5},{2,6},{3,7},{4,0},{5,1},{6,2},{7,3}} | collective-permute-start | bytes 1572872 | tf_op jit(solution)/shard_map/ppermute | solution.py:526
  164.6 45.8 %collective-permute-start.1 = (f32[4,128,256]{2,1,0:T(8,128)S(1)}, f32[4,128,256]{2,1,0:T(8,128)S(1)}, u32[]{:S(2)}, u32[]{:S(2)}) collective-permute-start(f32[4,128,256]{2,1,0:T(8,128)S(1)} %convert_add_fusion), channel_id=1, source_target_pairs={{0,2},{1,3},{2,0},{3,1},{4,6},{5,7},{6,4},{7,5}} | collective-permute-start | bytes 1572872 | tf_op jit(solution)/shard_map/ppermute | solution.py:526
  177.2 36.4 %copy-start.4 = (f32[128,3072]{1,0:T(8,128)}, f32[128,3072]{1,0:T(8,128)S(1)}, u32[]{:S(2)}) copy-start(f32[128,3072]{1,0:T(8,128)S(1)} %get-tuple-element.45.pa_ref) | copy-start | bytes 4718596
  177.2 36.4 %copy-start.6 = (f32[128,3072]{1,0:T(8,128)}, f32[128,3072]{1,0:T(8,128)S(1)}, u32[]{:S(2)}) copy-start(f32[128,3072]{1,0:T(8,128)S(1)} %get-tuple-element.46.pb_ref) | copy-start | bytes 4718596
  177.2 105.2 %collective-permute-start.5 = (f32[128,3072]{1,0:T(8,128)}, f32[128,3072]{1,0:T(8,128)}, u32[]{:S(2)}, u32[]{:S(2)}) collective-permute-start(f32[128,3072]{1,0:T(8,128)} %get-tuple-element.48), channel_id=1, source_target_pairs={{0,2},{1,3},{2,0},{3,1},{4,6},{5,7},{6,4},{7,5}} | collective-permute-start | bytes 4718600 | tf_op jit(solution)/shard_map/ppermute | solution.py:526
  210.1 36.4 %collective-permute-start.3 = (f32[2,128,256]{2,1,0:T(8,128)S(1)}, f32[2,128,256]{2,1,0:T(8,128)S(1)}, u32[]{:S(2)}, u32[]{:S(2)}) collective-permute-start(f32[2,128,256]{2,1,0:T(8,128)S(1)} %slice.84), channel_id=1, source_target_pairs={{0,2},{1,3},{2,0},{3,1},{4,6},{5,7},{6,4},{7,5}} | collective-permute-start | bytes 786440 | tf_op jit(solution)/shard_map/ppermute | solution.py:526
  210.5 37.1 %collective-permute-start.4 = (f32[2,128,256]{2,1,0:T(8,128)S(1)}, f32[2,128,256]{2,1,0:T(8,128)S(1)}, u32[]{:S(2)}, u32[]{:S(2)}) collective-permute-start(f32[2,128,256]{2,1,0:T(8,128)S(1)} %slice.93), channel_id=1, source_target_pairs={{0,4},{1,5},{2,6},{3,7},{4,0},{5,1},{6,2},{7,3}} | collective-permute-start | bytes 786440 | tf_op jit(solution)/shard_map/ppermute | solution.py:526
  212.2 2.0 copy-start.18
  213.6 68.8 %collective-permute-start.8 = (f32[128,3072]{1,0:T(8,128)}, f32[128,3072]{1,0:T(8,128)}, u32[]{:S(2)}, u32[]{:S(2)}) collective-permute-start(f32[128,3072]{1,0:T(8,128)} %add.83), channel_id=1, source_target_pairs={{0,4},{1,5},{2,6},{3,7},{4,0},{5,1},{6,2},{7,3}} | collective-permute-start | bytes 4718600 | tf_op jit(solution)/shard_map/ppermute | solution.py:526
  214.2 4.6 %copy-start.2 = (bf16[1024,6144]{1,0:T(8,128)(2,1)S(1)}, bf16[1024,6144]{1,0:T(8,128)(2,1)}, u32[]{:S(2)}) copy-start(bf16[1024,6144]{1,0:T(8,128)(2,1)} %get-tuple-element.55.x_ref) | copy-start | bytes 37748740
  233.4 52.0 %collective-permute-start.9 = (f32[128,3072]{1,0:T(8,128)}, f32[128,3072]{1,0:T(8,128)}, u32[]{:S(2)}, u32[]{:S(2)}) collective-permute-start(f32[128,3072]{1,0:T(8,128)} %get-tuple-element.52), channel_id=1, source_target_pairs={{0,4},{1,5},{2,6},{3,7},{4,0},{5,1},{6,2},{7,3}} | collective-permute-start | bytes 4718600 | tf_op jit(solution)/shard_map/ppermute | solution.py:526
  236.2 12.4 %copy-start.17 = (bf16[1024,768]{1,0:T(8,128)(2,1)S(1)}, bf16[1024,768]{1,0:T(8,128)(2,1)}, u32[]{:S(2)}) copy-start(bf16[1024,768]{1,0:T(8,128)(2,1)} %copy-done.16) | copy-start | bytes 4718596
  246.5 39.0 %collective-permute-start.11 = (f32[128,3072]{1,0:T(8,128)}, f32[128,3072]{1,0:T(8,128)}, u32[]{:S(2)}, u32[]{:S(2)}) collective-permute-start(f32[128,3072]{1,0:T(8,128)} %add.86), channel_id=1, source_target_pairs={{0,2},{1,3},{2,0},{3,1},{4,6},{5,7},{6,4},{7,5}} | collective-permute-start | bytes 4718600 | tf_op jit(solution)/shard_map/ppermute | solution.py:526
  248.6 25.3 %collective-permute-start.12 = (f32[4,128,256]{2,1,0:T(8,128)}, f32[4,128,256]{2,1,0:T(8,128)}, u32[]{:S(2)}, u32[]{:S(2)}) collective-permute-start(f32[4,128,256]{2,1,0:T(8,128)} %pad_maximum_fusion.1.sum_ref.mine_ref), channel_id=1, source_target_pairs={{0,1},{1,0},{2,3},{3,2},{4,5},{5,4},{6,7},{7,6}} | collective-permute-start | bytes 1572872 | tf_op jit(solution)/shard_map/ppermute | solution.py:526
  248.6 4.6 %copy-start.9 = (bf16[1024,6144]{1,0:T(8,128)(2,1)S(1)}, bf16[1024,6144]{1,0:T(8,128)(2,1)}, u32[]{:S(2)}) copy-start(bf16[1024,6144]{1,0:T(8,128)(2,1)} %get-tuple-element.58.dy_ref) | copy-start | bytes 37748740
  253.2 14.8 %copy-start = (bf16[6144,1,128]{2,0,1:T(8,128)(2,1)S(1)}, bf16[6144,1,128]{2,0,1:T(8,128)(2,1)}, u32[]{:S(2)}) copy-start(bf16[6144,1,128]{2,0,1:T(8,128)(2,1)} %param.9) | copy-start | bytes 4718596
  253.2 14.8 %copy-start.1 = (bf16[6144,1,128]{2,0,1:T(8,128)(2,1)S(1)}, bf16[6144,1,128]{2,0,1:T(8,128)(2,1)}, u32[]{:S(2)}) copy-start(bf16[6144,1,128]{2,0,1:T(8,128)(2,1)} %param.10) | copy-start | bytes 4718596
  268.0 1.4 copy-start.5
  269.4 1.4 copy-start.7
  274.0 4.6 %copy-start.3 = (bf16[1024,6144]{1,0:T(8,128)(2,1)S(1)}, bf16[1024,6144]{1,0:T(8,128)(2,1)}, u32[]{:S(2)}) copy-start(bf16[1024,6144]{1,0:T(8,128)(2,1)} %get-tuple-element.55.x_ref) | copy-start | bytes 37748740
  (3 other events, 2.8 us)

commit v2 on v1

--- a/solution.py
+++ b/solution.py
@@ -14,6 +14,7 @@
 VM = pl.BlockSpec(memory_space=pltpu.VMEM)
 BLK = 128
 HALF = 64
+FULL = 67043328
 CHUNK = 256
 X_NBR, Y_NBR, SIB = 2, 4, 1
 
@@ -60,11 +61,15 @@
             lax.fori_loop(0, n_heads, head, 0)
 
 
-def gather_kernel(
+def front_kernel(
     n_heads, scale,
     x_ref, dy_ref, wq_ref, wk_ref, wv_ref, wo_ref,
-    xf_ref, dyf_ref, wqs_ref, q_ref, k_ref, v_ref, do_ref, dqm_ref, dqs_ref, o_ref, dk_ref, dv_ref,
-    xb, yb, wq, wkv, wo, dq_tmp, send_sem, recv_sem, wsend, wrecv, lsem, osem,
+    xf_ref, dyf_ref, wqs_ref, pd_ref, r_ref, pxa_ref, pxb_ref, pya_ref, pyb_ref, poa_ref, pob_ref,
+    of_ref, dqf_ref, kvo_ref, kx0_ref, kx1_ref, ky0_ref, ky1_ref,
+    xb, yb, wq, wkv, wo, q_ref, do_ref, o_ref, dq_ref, k_ref, v_ref, dk_ref, dv_ref,
+    wt, pt, rt, got_q, dkv, got_kv, kvs,
+    send_sem, recv_sem, wsem, lsem, osem, gq_send, gq_recv, gkv_send, gkv_recv,
+    r_send, r_recv, kn_send, kn_recv, wt_sem, pt_sem, rt_sem, att_sem,
 ):
     me = lax.axis_index("tp")
     chip = me // 2
@@ -81,33 +86,26 @@
     counts = [0, 0]
     sends = []
 
+    def remote(src, dst, ssem, rsem, mask):
+        return pltpu.make_async_remote_copy(
+            src_ref=src, dst_ref=dst, send_sem=ssem, recv_sem=rsem,
+            device_id={"tp": partner[mask]}, device_id_type=MESH,
+        )
+
     def part(t, block, half):
         return bufs[t].at[block, pl.ds(half * HALF, HALF)]
 
     def send(t, block, half, mask, own=False):
         src = srcs[t].at[pl.ds(half * HALF, HALF)] if own else part(t, block, half)
-        copy = pltpu.make_async_remote_copy(
-            src_ref=src,
-            dst_ref=part(t, block, half),
-            send_sem=send_sem.at[t, counts[t]],
-            recv_sem=recv_sem.at[t, block, half],
-            device_id={"tp": partner[mask]},
-            device_id_type=MESH,
-        )
+        copy = remote(src, part(t, block, half), send_sem.at[t, counts[t]], recv_sem.at[t, block, half], mask)
         counts[t] += 1
         copy.start()
         sends.append(copy)
 
     def arrive(t, mask, half):
         block = partner[mask]
-        pltpu.make_async_remote_copy(
-            src_ref=part(t, block, half),
-            dst_ref=part(t, block, half),
-            send_sem=send_sem.at[t, 0],
-            recv_sem=recv_sem.at[t, block, half],
-            device_id={"tp": partner[SIB]},
-            device_id_type=MESH,
-        ).wait_recv()
+        here = part(t, block, half)
+        remote(here, here, send_sem.at[t, 0], recv_sem.at[t, block, half], SIB).wait_recv()
 
     for half in range(2):
         send(0, me, half, X_NBR, own=True)
@@ -128,10 +126,7 @@
         send(0, me, half, SIB, own=True)
     for half in range(2):
         send(1, me, half, SIB, own=True)
-    w_copy = pltpu.make_async_remote_copy(
-        src_ref=wq_ref, dst_ref=wqs_ref, send_sem=wsend, recv_sem=wrecv,
-        device_id={"tp": partner[SIB]}, device_id_type=MESH,
-    )
+    w_copy = remote(wq_ref, wqs_ref, wsem.at[0], wsem.at[1], SIB)
     w_copy.start()
     dk_ref[...] = jnp.zeros_like(dk_ref)
     dv_ref[...] = jnp.zeros_like(dv_ref)
@@ -140,6 +135,9 @@
 
     def chunk_of(p):
         return jnp.bitwise_xor(chip, p)
+
+    def block_rows(p, cls):
+        return pl.ds(pl.multiple_of(chunk_of(p) * CHUNK + cls * BLK, BLK), BLK)
 
     def write_out(t, p):
         chunk = chunk_of(p)
@@ -184,6 +182,51 @@
     def both(t, mask):
         arrive(t, mask, 0)
         arrive(t, mask, 1)
+
+    def attend_rows(p):
+        chunk = chunk_of(p)
+        rows = rows_of(chunk)
+
+        def put(h, o, dq):
+            cols = pl.ds(pl.multiple_of(h * BLK, BLK), BLK)
+            o_ref[rows, cols] = o
+            dq_ref[rows, cols] = dq
+
+        attend_chunk(chunk, n_heads, scale, q_ref, do_ref, k_ref, v_ref, put, dk_ref, dv_ref)
+
+    def att_out(p):
+        rows = rows_of(chunk_of(p))
+        return (
+            pltpu.make_async_copy(o_ref.at[rows], of_ref.at[rows], att_sem.at[p, 0]),
+            pltpu.make_async_copy(dq_ref.at[rows], dqf_ref.at[rows], att_sem.at[p, 1]),
+        )
+
+    def give_q(p):
+        return remote(dq_ref.at[block_rows(p, 1 - core)], got_q.at[p], gq_send.at[p], gq_recv.at[p], SIB)
+
+    def give_kv(p):
+        return remote(dkv.at[block_rows(p, 1 - core)], got_kv.at[p], gkv_send.at[p], gkv_recv.at[p], SIB)
+
+    tile = wt.shape[2]
+    steps = pd_ref.shape[1]
+
+    def w_load(side, i):
+        col = pl.multiple_of((side * steps + i) * tile, tile)
+        return pltpu.make_async_copy(wqs_ref.at[:, pl.ds(col, tile), :], wt.at[side], wt_sem.at[side])
+
+    def product(groups, side, i):
+        col = pl.multiple_of((side * steps + i) * tile, tile)
+        lhs = jnp.concatenate(
+            [
+                jnp.concatenate([dq_ref[block_rows(p, core), :] for p in groups], axis=0),
+                jnp.concatenate([got_q[p] for p in groups], axis=0),
+            ],
+            axis=1,
+        )
+        rhs = jnp.concatenate(
+            [wq[h, pl.ds(col, tile), :] for h in range(n_heads)] + [wt[side, h] for h in range(n_heads)], axis=1
+        )
+        return mm(lhs, rhs, 1, 1)
 
     for copy in loads[:4]:
         copy.wait()
@@ -226,17 +269,47 @@
         else:
             project_out(3)
 
-    chunk_d = chunk_of(3)
-
-    def put(h, o, dq):
-        cols = pl.ds(pl.multiple_of(h * BLK, BLK), BLK)
-        o_ref[:, cols] = o
-        dq_tmp[0, :, cols] = dq[:BLK]
-        dq_tmp[1, :, cols] = dq[BLK:]
-
-    attend_chunk(chunk_d, n_heads, scale, q_ref, do_ref, k_ref, v_ref, put, dk_ref, dv_ref)
-    dqm_ref[...] = dq_tmp[core]
-    dqs_ref[...] = dq_tmp[1 - core]
+    attend_rows(3)
+    give_q(3).start()
+    w_copy.wait()
+    for side in range(2):
+        w_load(side, 0).start()
+    for copy in att_out(3):
+        copy.start()
+    give_q(3).wait_recv()
+
+    def pd_write(side, i):
+        return pltpu.make_async_copy(pt.at[side, pl.ds(0, BLK)], pd_ref.at[side, i], pt_sem.at[side, 0])
+
+    def round1(side, i):
+        mask = (X_NBR, Y_NBR)[side]
+        return remote(pd_ref.at[side, i], r_ref.at[side, i], r_send.at[side, i], r_recv.at[side, i], mask)
+
+    def pd_step(i, carry):
+        for side in range(2):
+            w_load(side, i).wait()
+            res = product((3,), side, i)
+
+            @pl.when(i > 0)
+            def _(side=side):
+                pd_write(side, i - 1).wait()
+                round1(side, i - 1).start()
+
+            pt[side, :BLK] = res
+            pd_write(side, i).start()
+
+            @pl.when(i < steps - 1)
+            def _(side=side):
+                w_load(side, i + 1).start()
+
+        return carry
+
+    lax.fori_loop(0, steps, pd_step, 0)
+    for side in range(2):
+        pd_write(side, steps - 1).wait()
+        round1(side, steps - 1).start()
+        w_load(side, 0).start()
+
     arrive(1, X_NBR, 1)
     send(1, partner[X_NBR], 1, SIB)
     arrive(1, Y_NBR, 0)
@@ -245,144 +318,146 @@
     project_out(1)
     both(1, Y_NBR ^ SIB)
     project_out(2)
+
+    def rest(i, carry):
+        p = lax.rem(i + 1, 3)
+        attend_rows(p)
+        give_q(p).start()
+        for copy in att_out(p):
+            copy.start()
+        return carry
+
+    lax.fori_loop(0, 3, rest, 0)
+    dkv[:, :BLK] = (dk_ref[...] * scale).astype(BF16)
+    dkv[:, BLK:] = dv_ref[...].astype(BF16)
+    for p in range(3):
+        give_q(p).wait_recv()
+    for p in range(4):
+        give_kv(p).start()
+
+    def r_load(side, i):
+        return pltpu.make_async_copy(r_ref.at[side, i], rt.at[side], rt_sem.at[side])
+
+    groups = (1, 2, 0)
+    targets = ((pxa_ref, pya_ref, poa_ref), (pxb_ref, pyb_ref, pob_ref))
+
+    def p_writes(side, i):
+        return [
+            pltpu.make_async_copy(pt.at[side, pl.ds(g * BLK, BLK)], targets[side][g].at[i], pt_sem.at[side, g])
+            for g in range(3)
+        ]
+
+    def p_step(i, carry):
+        for side in range(2):
+            round1(side, i).wait_recv()
+            r_load(side, i).start()
+            w_load(side, i).wait()
+            res = product(groups, side, i)
+
+            @pl.when(i > 0)
+            def _(side=side):
+                for copy in p_writes(side, i - 1):
+                    copy.wait()
+
+            r_load(side, i).wait()
+            add = 1 - side
+            for g in range(3):
+                rows = res[g * BLK : (g + 1) * BLK]
+                pt[side, g * BLK : (g + 1) * BLK] = rows + rt[side] if g == add else rows
+            for copy in p_writes(side, i):
+                copy.start()
+
+            @pl.when(i < steps - 1)
+            def _(side=side):
+                w_load(side, i + 1).start()
+
+        return carry
+
+    for p in range(4):
+        give_kv(p).wait_recv()
+        kvs[p] = dkv[block_rows(p, core), :].astype(F32) + got_kv[p].astype(F32)
+    p_step(0, 0)
+    near = [
+        remote(kvs.at[pl.ds(2 * i, 2)], dst, kn_send.at[n, i], kn_recv.at[n, i], mask)
+        for n, (mask, dsts) in enumerate(((X_NBR, (kx0_ref, kx1_ref)), (Y_NBR, (ky0_ref, ky1_ref))))
+        for i, dst in enumerate(dsts)
+    ]
+    for copy in near:
+        copy.start()
+    kv_out = pltpu.make_async_copy(kvs, kvo_ref, lsem.at[0])
+    kv_out.start()
+    lax.fori_loop(1, steps, p_step, 0)
+    for side in range(2):
+        for copy in p_writes(side, steps - 1):
+            copy.wait()
     for copy in sends:
         copy.wait_send()
-    w_copy.wait()
+    for p in range(4):
+        give_q(p).wait_send()
+        give_kv(p).wait_send()
+        for copy in att_out(p):
+            copy.wait()
+    for side in range(2):
+        for i in range(steps):
+            round1(side, i).wait_send()
+    for copy in near:
+        copy.wait()
+    kv_out.wait()
     for copy in writes:
         copy.wait()
 
 
-def gather_project(x_blk, dy_blk, wq, wk, wv, wo, n_dev, scale):
+TILE = 512
+
+
+def front(x_blk, dy_blk, wq, wk, wv, wo, n_dev, scale):
     n_heads, dim, hd = wq.shape
     tokens = x_blk.shape[0] * n_dev
     wide = n_heads * hd
+    steps = dim // 2 // TILE
     sds = jax.ShapeDtypeStruct
+    sem = pltpu.SemaphoreType.DMA
+    piece = sds((steps, BLK, TILE), F32)
     return pl.pallas_call(
-        functools.partial(gather_kernel, n_heads, scale),
+        functools.partial(front_kernel, n_heads, scale),
         out_shape=(
             sds((tokens, dim), BF16), sds((tokens, dim), BF16), sds(wq.shape, BF16),
-            sds((tokens, wide), BF16), sds((tokens, hd), BF16), sds((tokens, hd), BF16), sds((tokens, wide), BF16),
-            sds((BLK, wide), BF16), sds((BLK, wide), BF16), sds((CHUNK, wide), BF16),
-            sds((tokens, hd), F32), sds((tokens, hd), F32),
-        ),
+            sds((2, steps, BLK, TILE), F32), sds((2, steps, BLK, TILE), F32),
+            piece, piece, piece, piece, piece, piece,
+            sds((tokens, wide), BF16), sds((tokens, wide), BF16), sds((4, BLK, 2 * hd), F32),
+        )
+        + (sds((2, BLK, 2 * hd), F32),) * 4,
         in_specs=[ANY] * 6,
-        out_specs=(ANY,) * 3 + (VM,) * 9,
+        out_specs=(ANY,) * 18,
         scratch_shapes=[
             pltpu.VMEM((n_dev, BLK, dim), BF16),
             pltpu.VMEM((n_dev, BLK, dim), BF16),
             pltpu.VMEM(wq.shape, BF16),
             pltpu.VMEM((2, dim, hd), BF16),
             pltpu.VMEM(wo.shape, BF16),
-            pltpu.VMEM((2, BLK, wide), BF16),
-            pltpu.SemaphoreType.DMA((2, 14)),
-            pltpu.SemaphoreType.DMA((2, n_dev, 2)),
-            pltpu.SemaphoreType.DMA,
-            pltpu.SemaphoreType.DMA,
-            pltpu.SemaphoreType.DMA((6,)),
-            pltpu.SemaphoreType.DMA((2, 4, 2)),
+            pltpu.VMEM((tokens, wide), BF16),
+            pltpu.VMEM((tokens, wide), BF16),
+            pltpu.VMEM((tokens, wide), BF16),
+            pltpu.VMEM((tokens, wide), BF16),
+            pltpu.VMEM((tokens, hd), BF16),
+            pltpu.VMEM((tokens, hd), BF16),
+            pltpu.VMEM((tokens, hd), F32),
+            pltpu.VMEM((tokens, hd), F32),
+            pltpu.VMEM((2, n_heads, TILE, hd), BF16),
+            pltpu.VMEM((2, 3 * BLK, TILE), F32),
+            pltpu.VMEM((2, BLK, TILE), F32),
+            pltpu.VMEM((4, BLK, wide), BF16),
+            pltpu.VMEM((tokens, 2 * hd), BF16),
+            pltpu.VMEM((4, BLK, 2 * hd), BF16),
+            pltpu.VMEM((4, BLK, 2 * hd), F32),
+            sem((2, 14)), sem((2, n_dev, 2)), sem((2,)), sem((6,)), sem((2, 4, 2)),
+            sem((4,)), sem((4,)), sem((4,)), sem((4,)),
+            sem((2, steps)), sem((2, steps)), sem((2, 2)), sem((2, 2)),
+            sem((2,)), sem((2, 3)), sem((2,)), sem((4, 2)),
         ],
-        compiler_params=pltpu.CompilerParams(
-            collective_id=0, has_side_effects=True, vmem_limit_bytes=67043328
-        ),
-        name="gather_project",
+        compiler_params=pltpu.CompilerParams(collective_id=0, has_side_effects=True, vmem_limit_bytes=FULL),
+        name="front",
     )(x_blk, dy_blk, wq, wk, wv, wo)
-
-
-def attend_kernel(
-    n_heads, scale,
-    q_ref, k_ref, v_ref, do_ref, od_ref, dqd_ref, dqs_ref, dk0_ref, dv0_ref,
-    o_ref, dq_ref, mine_ref, give_ref, dk_ref, dv_ref,
-):
-    me = lax.axis_index("tp")
-    chip = me // 2
-    core = lax.rem(me, 2)
-    wide = q_ref.shape[1]
-    dk_ref[...] = dk0_ref[...]
-    dv_ref[...] = dv0_ref[...]
-
-    def step(i, carry):
-        chunk = jnp.bitwise_xor(chip, lax.rem(i + 1, 3))
-        rows = rows_of(chunk)
-
-        def put(h, o, dq):
-            cols = pl.ds(pl.multiple_of(h * BLK, BLK), BLK)
-            o_ref[rows, cols] = o
-            dq_ref[rows, cols] = dq
-
-        attend_chunk(chunk, n_heads, scale, q_ref, do_ref, k_ref, v_ref, put, dk_ref, dv_ref)
-        return carry
-
-    lax.fori_loop(0, 3, step, 0)
-    chunk_d = jnp.bitwise_xor(chip, 3)
-    o_ref[rows_of(chunk_d), :] = od_ref[...]
-    dq_ref[pl.ds(pl.multiple_of(chunk_d * CHUNK + core * BLK, BLK), BLK), :] = dqd_ref[...]
-    dq_ref[pl.ds(pl.multiple_of(chunk_d * CHUNK + (1 - core) * BLK, BLK), BLK), :] = dqs_ref[...]
-    for p in range(4):
-        chunk = jnp.bitwise_xor(chip, p)
-        for ref, cls in ((mine_ref, core), (give_ref, 1 - core)):
-            rows = pl.ds(pl.multiple_of(chunk * CHUNK + cls * BLK, BLK), BLK)
-            ref[p, :, :wide] = dq_ref[rows, :]
-            ref[p, :, wide : wide + BLK] = (dk_ref[rows, :] * scale).astype(BF16)
-            ref[p, :, wide + BLK :] = dv_ref[rows, :].astype(BF16)
-
-
-def attend(q, k, v, d_out, o_d, dqm_d, dqs_d, dk0, dv0, n_heads, scale):
-    tokens, wide = q.shape
-    hd = k.shape[1]
-    sds = jax.ShapeDtypeStruct
-    pairs = tokens * tokens * n_heads // 2
-    return pl.pallas_call(
-        functools.partial(attend_kernel, n_heads, scale),
-        out_shape=(
-            sds((tokens, wide), BF16), sds((tokens, wide), BF16),
-            sds((4, BLK, wide + 2 * hd), BF16), sds((4, BLK, wide + 2 * hd), BF16),
-        ),
-        in_specs=[VM] * 9,
-        out_specs=(VM,) * 4,
-        scratch_shapes=[pltpu.VMEM((tokens, hd), F32), pltpu.VMEM((tokens, hd), F32)],
-        compiler_params=pltpu.CompilerParams(vmem_limit_bytes=48 * 2**20),
-        cost_estimate=pl.CostEstimate(flops=pairs * hd * 24, bytes_accessed=12 * 2**20, transcendentals=pairs),
-        name="attend",
-    )(q, k, v, d_out, o_d, dqm_d, dqs_d, dk0, dv0)
-
-
-def dx_kernel(groups, wide, mine_ref, got_ref, wa_ref, wb_ref, sa_ref, sb_ref, *out_refs):
-    lhs = jnp.concatenate(
-        [
-            jnp.concatenate([mine_ref[g, :, :wide] for g in groups], axis=0),
-            jnp.concatenate([got_ref[g, :, :wide] for g in groups], axis=0),
-        ],
-        axis=1,
-    )
-    for side, (w_ref, s_ref) in enumerate(((wa_ref, sa_ref), (wb_ref, sb_ref))):
-        n = w_ref.shape[0]
-        rhs = jnp.concatenate([w_ref[h] for h in range(n)] + [s_ref[h] for h in range(n)], axis=1)
-        res = mm(lhs, rhs, 1, 1)
-        for i in range(len(groups)):
-            out_refs[2 * i + side][...] = res[i * BLK : (i + 1) * BLK]
-
-
-def dx_partial(mine, got, wq, wqs, groups):
-    n_heads, dim, hd = wq.shape
-    tile = 512
-    half = dim // 2
-    steps = half // tile
-    rows = BLK * len(groups)
-    w_lo = pl.BlockSpec((n_heads, tile, hd), lambda j: (0, j, 0))
-    w_hi = pl.BlockSpec((n_heads, tile, hd), lambda j: (0, j + steps, 0))
-    whole = pl.BlockSpec(mine.shape, lambda j: (0, 0, 0))
-    return pl.pallas_call(
-        functools.partial(dx_kernel, groups, n_heads * hd),
-        grid=(steps,),
-        out_shape=(jax.ShapeDtypeStruct((BLK, half), F32),) * (2 * len(groups)),
-        in_specs=[whole, whole, w_lo, w_hi, w_lo, w_hi],
-        out_specs=(pl.BlockSpec((BLK, tile), lambda j: (0, j)),) * (2 * len(groups)),
-        compiler_params=pltpu.CompilerParams(vmem_limit_bytes=40 * 2**20),
-        cost_estimate=pl.CostEstimate(
-            flops=4 * rows * dim * n_heads * hd, bytes_accessed=4 * dim * n_heads * hd + 4 * rows * dim, transcendentals=0
-        ),
-        name="dx_partial",
-    )(mine, got, wq, wq, wqs, wqs)
 
 
 def dwo_kernel(o_ref, dy_ref, out_ref, o_t):
@@ -407,7 +482,7 @@
         in_specs=[pl.BlockSpec((tokens, wide), lambda j: (0, 0)), pl.BlockSpec((tokens, tile), lambda j: (0, j))],
         out_specs=pl.BlockSpec((n_heads, BLK, tile), lambda j: (0, 0, j)),
         scratch_shapes=[pltpu.VMEM((wide, tokens), BF16)],
-        compiler_params=pltpu.CompilerParams(vmem_limit_bytes=40 * 2**20),
+        compiler_params=pltpu.CompilerParams(vmem_limit_bytes=FULL),
         cost_estimate=pl.CostEstimate(
             flops=2 * tokens * wide * dim, bytes_accessed=2 * tokens * dim + 4 * wide * dim, transcendentals=0
         ),
@@ -432,7 +507,7 @@
         out_shape=jax.ShapeDtypeStruct((n_heads, dim, BLK), F32),
         in_specs=[pl.BlockSpec((tokens, tile), lambda j: (0, j)), pl.BlockSpec((tokens, wide), lambda j: (0, 0))],
         out_specs=pl.BlockSpec((n_heads, tile, BLK), lambda j: (0, j, 0)),
-        compiler_params=pltpu.CompilerParams(vmem_limit_bytes=40 * 2**20),
+        compiler_params=pltpu.CompilerParams(vmem_limit_bytes=FULL),
         cost_estimate=pl.CostEstimate(
             flops=2 * tokens * wide * dim, bytes_accessed=2 * tokens * dim + 4 * wide * dim, transcendentals=0
         ),
@@ -480,7 +555,7 @@
             scratch_shapes=[pltpu.VMEM((tokens, 3 * mine.shape[2]), BF16)],
         ),
         out_shape=(jax.ShapeDtypeStruct((own, BLK), F32),) * 2,
-        compiler_params=pltpu.CompilerParams(vmem_limit_bytes=40 * 2**20),
+        compiler_params=pltpu.CompilerParams(vmem_limit_bytes=FULL),
         cost_estimate=pl.CostEstimate(
             flops=2 * tokens * own * 3 * mine.shape[2], bytes_accessed=4 * tokens * own, transcendentals=0
         ),
@@ -501,22 +576,48 @@
 
 def kv_dx(total, wk, wv, pa, pb):
     dim, hd = wk.shape
-    half = dim // 2
-    tile = 1024
-    steps = half // tile
+    steps, _, tile = pa.shape
     w_lo = pl.BlockSpec((tile, hd), lambda j: (j, 0))
     w_hi = pl.BlockSpec((tile, hd), lambda j: (j + steps, 0))
-    col = pl.BlockSpec((BLK, tile), lambda j: (0, j))
+    col = pl.BlockSpec((None, BLK, tile), lambda j: (j, 0, 0))
     return pl.pallas_call(
         kvdx_kernel,
         grid=(steps,),
-        out_shape=(jax.ShapeDtypeStruct((BLK, half), F32),) * 2,
+        out_shape=(jax.ShapeDtypeStruct(pa.shape, F32),) * 2,
         in_specs=[pl.BlockSpec((1,) + total.shape[1:], lambda j: (0, 0, 0)), w_lo, w_hi, w_lo, w_hi, col, col],
         out_specs=(col, col),
-        compiler_params=pltpu.CompilerParams(vmem_limit_bytes=40 * 2**20),
+        compiler_params=pltpu.CompilerParams(vmem_limit_bytes=FULL),
         cost_estimate=pl.CostEstimate(flops=12 * BLK * dim * hd, bytes_accessed=10 * 2**20, transcendentals=0),
         name="kv_dx",
     )(total, wk, wk, wv, wv, pa, pb)
+
+
+def dx_sum_kernel(steps, a0, a1, a2, b0, b1, b2, out_ref):
+    j = pl.program_id(0)
+
+    @pl.when(j < steps)
+    def _():
+        out_ref[...] = ((a0[...] + a1[...]) + a2[...]).astype(BF16)
+
+    @pl.when(j >= steps)
+    def _():
+        out_ref[...] = ((b0[...] + b1[...]) + b2[...]).astype(BF16)
+
+
+def dx_sum(a_terms, b_terms):
+    steps, _, tile = a_terms[0].shape
+    a_spec = pl.BlockSpec((None, BLK, tile), lambda j: (jnp.minimum(j, steps - 1), 0, 0))
+    b_spec = pl.BlockSpec((None, BLK, tile), lambda j: (jnp.maximum(j - steps, 0), 0, 0))
+    return pl.pallas_call(
+        functools.partial(dx_sum_kernel, steps),
+        grid=(2 * steps,),
+        out_shape=jax.ShapeDtypeStruct((BLK, 2 * steps * tile), BF16),
+        in_specs=[a_spec] * 3 + [b_spec] * 3,
+        out_specs=pl.BlockSpec((BLK, tile), lambda j: (0, j)),
+        compiler_params=pltpu.CompilerParams(vmem_limit_bytes=FULL),
+        cost_estimate=pl.CostEstimate(flops=2**20, bytes_accessed=12 * 2**20, transcendentals=0),
+        name="dx_sum",
+    )(*a_terms, *b_terms)
 
 
 def solution(mesh):
@@ -533,31 +634,25 @@
         wk = w_k[:, 0, :]
         wv = w_v[:, 0, :]
         me = lax.axis_index("tp").astype(jnp.int32).reshape(1)
-        xf, dyf, wqs, q, k, v, d_out, dqm_d, dqs_d, o_d, dk0, dv0 = gather_project(
-            x_blk, dy_blk, wq, wk, wv, wo_loc, n_dev, scale
-        )
-        dqg_d = swap(dqs_d, SIB)
-        pd_a, pd_b = dx_partial(dqm_d[None], dqg_d[None], wq, wqs, (0,))
-        ra = swap(pd_a, X_NBR)
-        rb = swap(pd_b, Y_NBR)
-        o, dq, mine, give = attend(q, k, v, d_out, o_d, dqm_d, dqs_d, dk0, dv0, n_heads, scale)
-        got = swap(give, SIB)
-        kvs = mine[:, :, wide:].astype(F32) + got[:, :, wide:].astype(F32)
-        kv_x = swap(kvs, X_NBR)
-        kv_y = swap(kvs, Y_NBR)
-        px_a, px_b, py_a, py_b, po_a, po_b = dx_partial(mine, got, wq, wqs, (1, 2, 0))
+        (
+            xf, dyf, _, _, _, px_a, px_b, py_a, py_b, po_a, po_b, o, dq, kvs, kx0, kx1, ky0, ky1
+        ) = front(x_blk, dy_blk, wq, wk, wv, wo_loc, n_dev, scale)
+        kd0 = swap(kx0, Y_NBR)
+        kd1 = swap(ky1, X_NBR)
         a2 = swap(px_a, X_NBR)
         b2 = swap(py_b, Y_NBR)
-        kv_d = jnp.concatenate([swap(kv_x[:2], Y_NBR), swap(kv_y[2:], X_NBR)], axis=0)
+        a3 = swap(py_a, Y_NBR)
+        b3 = swap(px_b, X_NBR)
         dwo = grad_wo(o, dyf)
-        a3 = swap(py_a + ra, Y_NBR)
-        b3 = swap(px_b + rb, X_NBR)
+        kv_x = (kx0[0], kx0[1], kx1[0], kx1[1])
+        kv_y = (ky0[0], ky0[1], ky1[0], ky1[1])
+        kv_d = (kd0[0], kd0[1], kd1[0], kd1[1])
         total = jnp.stack([kvs[p] + kv_x[p ^ 1] + kv_y[p ^ 2] + kv_d[p ^ 3] for p in range(4)])
         other = swap(total, SIB)
         dwq = grad_wq(xf, dq)
         base_a, base_b = kv_dx(total, wk, wv, po_a, po_b)
         dwk, dwv = grad_kv(me, total, other, xf, n_dev)
-        dx = jnp.concatenate([(base_a + a2) + a3, (base_b + b2) + b3], axis=1).astype(BF16)
+        dx = dx_sum((base_a, a2, a3), (base_b, b2, b3))
         return dx, jnp.transpose(dwq, (1, 0, 2)), dwo, dwk, dwv
 
     tok_spec = P(("dp", "tp"))

time: 290 us -> 255 us (0.88)
  Pallas kernels: 199 us -> 227 us
  waiting for transfers between devices: 42.2 us -> 17.6 us
  local copies, waits for them, and re-layouts: 24.2 us -> 0 us
  starting transfers between devices: 13.3 us -> 5.17 us
  other arithmetic: 9.3 us -> 2.57 us
    ppermute x13 -> x7, waiting for transfers between devices: 42.2 us -> 17.6 us  [swap(): return lax.ppermute(a, 'tp', [(i, i ^ mask) for i in range(n_dev)])]
    unnamed x44 -> x0, local copies, waits for them, and re-layouts: 24.2 us -> none
    pallas_call x4 -> x2, Pallas kernels: 163 us -> 177 us  [the longest x1 168 us: front(): pl.pallas_call(functools.partial(front_kernel, n_heads, scale), out_shape...]
    ppermute x13 -> x7, starting transfers between devices: 13.3 us -> 5.17 us  [swap(): return lax.ppermute(a, 'tp', [(i, i ^ mask) for i in range(n_dev)])]
    pallas_call x1, Pallas kernels: 14.6 us -> 19.5 us  [grad_wq(): pl.pallas_call(dwq_kernel, grid=(dim // tile,), out_shape=jax.ShapeDtypeS...]
    pallas_call x1, Pallas kernels: 14.8 us -> 19.6 us  [grad_wo(): pl.pallas_call(dwo_kernel, grid=(dim // tile,), out_shape=jax.ShapeDtypeS...]
    another operation x2 -> x0, other arithmetic: 4.27 us -> none
    pallas_call x1, Pallas kernels: 3.13 us -> 7.01 us  [kv_dx(): pl.pallas_call(kvdx_kernel, grid=(steps,), out_shape=(jax.ShapeDtypeStruc...]
  transfers between devices with their start and end apart: 13 -> 7, of which waited for: 3 -> 2; matrix products, arithmetic and copies ran while one was open for 2% -> 1% of each run, Pallas kernels for 28% -> 20%
where the time goes in v2:
time: 255 us; the launch traced here: 253 us
  Pallas kernels  227 us (89%)
  waiting for transfers between devices  17.6 us (7%)
  starting transfers between devices  5.17 us (2%)
  other arithmetic  2.57 us (1%)
    pallas_call x1, Pallas kernels, front(): pl.pallas_call(functools.partial(front_kernel, n_heads, scale), out_shape...  168 us
    pallas_call x1, Pallas kernels, grad_wo(): pl.pallas_call(dwo_kernel, grid=(dim // tile,), out_shape=jax.ShapeDtypeS...  19.6 us
    pallas_call x1, Pallas kernels, grad_wq(): pl.pallas_call(dwq_kernel, grid=(dim // tile,), out_shape=jax.ShapeDtypeS...  19.5 us
    ppermute x7, waiting for transfers between devices, swap(): return lax.ppermute(a, 'tp', [(i, i ^ mask) for i in range(n_dev)])  17.6 us
    pallas_call x1, Pallas kernels, dx_sum(): pl.pallas_call(functools.partial(dx_sum_kernel, steps), grid=(2 * steps,)...  9.02 us
    pallas_call x1, Pallas kernels, kv_dx(): pl.pallas_call(kvdx_kernel, grid=(steps,), out_shape=(jax.ShapeDtypeStruc...  7.01 us
    ppermute x7, starting transfers between devices, swap(): return lax.ppermute(a, 'tp', [(i, i ^ mask) for i in range(n_dev)])  5.17 us
  transfers between devices with their start and end apart: 7, of which 2 were waited for; matrix products, arithmetic and copies ran while one was open for 1% of the time, Pallas kernels for 20%

profile of v2, /device:TPU:0, one launch (start us, length us, event | category | flops | bytes accessed | tf_op | source)
XLA Modules:
  0.0 253.2 jit_solution(18327148310752139782)
XLA Ops:
  0.6 167.6 %front.1 = (bf16[1024,6144]{1,0:T(8,128)(2,1)}, bf16[1024,6144]{1,0:T(8,128)(2,1)}, bf16[6,6144,128]{2,1,0:T(8,128)(2,1)}, f32[2,6,128,512]{3,2,1,0:T(8,128)}, f...) custom-call(bf16[128,6144]{1,0:T(8,128)(2,1)} %x_ref.1, ...), custom_call_target="tpu_custom_call" | custom-call | tf_op jit(solution)/shard_map/front/pallas_call | solution.py:421
  168.2 0.6 collective-permute-start
  168.8 1.5 collective-permute-start.1
  170.3 0.5 collective-permute-start.2
  170.8 1.5 collective-permute-start.3
  172.3 0.6 collective-permute-start.4
  172.9 4.6 %collective-permute-done = f32[2,128,256]{2,1,0:T(8,128)} collective-permute-done((f32[2,128,256]{2,1,0:T(8,128)}, f32[2,128,256]{2,1,0:T(8,128)}, u32[]{:S(2)}, u32[]{:S(2)}) %collective-permute-start) | collective-permute-done | bytes 262176 | tf_op jit(solution)/shard_map/ppermute | solution.py:627
  177.4 0.5 collective-permute-start.5
  178.0 19.5 %grad_wq.1 = f32[6,6144,128]{2,1,0:T(8,128)} custom-call(bf16[1024,6144]{1,0:T(8,128)(2,1)} %get-tuple-element.37.x_ref, bf16[1024,768]{1,0:T(8,128)(2,1)} %get-tuple-element.38.dq_ref), custom_call_target="tpu_custom_call" | custom-call | flops 9663676416 | bytes 31457280 | tf_op jit(solution)/shard_map/grad_wq/pallas_call | solution.py:504
  197.5 0.0 collective-permute-done.1
  197.5 1.7 slice_add_fusion.3
  199.2 0.8 pad_maximum_fusion.sum_ref.mine_ref
  200.1 0.0 collective-permute-start.6
  200.1 19.6 %grad_wo.1 = f32[6,128,6144]{2,1,0:T(8,128)} custom-call(bf16[1024,768]{1,0:T(8,128)(2,1)} %get-tuple-element.39.o_ref, bf16[1024,6144]{1,0:T(8,128)(2,1)} %get-tuple-element.40.dy_ref), custom_call_target="tpu_custom_call" | custom-call | flops 9663676416 | bytes 31457280 | tf_op jit(solution)/shard_map/grad_wo/pallas_call | solution.py:478
  219.7 7.0 %kv_dx.1 = (f32[6,128,512]{2,1,0:T(8,128)}, f32[6,128,512]{2,1,0:T(8,128)}) custom-call(f32[4,128,256]{2,1,0:T(8,128)} %pad_maximum_fusion.sum_ref.mine_ref, bf16[6144,128]{1,0:T(8,128)(2,1)} %bitcast.6, bf16[6144,128]{1,0:T(8,128)(2,1)} %bitcast.7, bf16[6144,128]{1,0:T(8,128)(2,1)} %bitcast.9, bf16[6144,128]{1,0:T(8,128)(2,1)} %bitcast.10, ...), custom_call_target="tpu_custom_call" | custom-call | flops 1207959552 | bytes 10485760 | tf_op jit(solution)/shard_map/kv_dx/pallas_call | solution.py:583
  226.7 0.0 collective-permute-done.6.other_ref
  226.7 4.4 %grad_kv.1 = (f32[768,128]{1,0:T(8,128)}, f32[768,128]{1,0:T(8,128)}) custom-call(s32[1]{0:T(128)} %bitcast.4.me_ref, f32[4,128,256]{2,1,0:T(8,128)} %pad_maximum_fusion.sum_ref.mine_ref, f32[4,128,256]{2,1,0:T(8,128)} %collective-permute-done.6.other_ref, bf16[1024,6144]{1,0:T(8,128)(2,1)} %get-tuple-element.37.x_ref), custom_call_target="tpu_custom_call" | custom-call | flops 1207959552 | bytes 3145728 | tf_op jit(solution)/shard_map/grad_kv/pallas_call | solution.py:548
  231.1 0.0 collective-permute-done.2.a1
  231.1 0.0 collective-permute-done.3.a2
  231.1 13.1 %collective-permute-done.4.b1 = f32[6,128,512]{2,1,0:T(8,128)} collective-permute-done((f32[6,128,512]{2,1,0:T(8,128)}, f32[6,128,512]{2,1,0:T(8,128)}, u32[]{:S(2)}, u32[]{:S(2)}) %collective-permute-start.4) | collective-permute-done | bytes 1572896 | tf_op jit(solution)/shard_map/ppermute | solution.py:627
  244.2 0.0 collective-permute-done.5.b2
  244.2 9.0 %dx_sum.1 = bf16[128,6144]{1,0:T(8,128)(2,1)} custom-call(f32[6,128,512]{2,1,0:T(8,128)} %get-tuple-element.31.a0, f32[6,128,512]{2,1,0:T(8,128)} %collective-permute-done.2.a1, f32[6,128,512]{2,1,0:T(8,128)} %collective-permute-done.3.a2, f32[6,128,512]{2,1,0:T(8,128)} %get-tuple-element.34.b0, f32[6,128,512]{2,1,0:T(8,128)} %collective-permute-done.4.b1, ...), custom_call_target="tpu_custom_call" | custom-call | flops 1048576 | bytes 12582912 | tf_op jit(solution)/shard_map/dx_sum/pallas_call | solution.py:611
Async XLA Ops:
  168.2 9.2 %collective-permute-start = (f32[2,128,256]{2,1,0:T(8,128)}, f32[2,128,256]{2,1,0:T(8,128)}, u32[]{:S(2)}, u32[]{:S(2)}) collective-permute-start(f32[2,128,256]{2,1,0:T(8,128)} %get-tuple-element.26), channel_id=1, source_target_pairs={{0,2},{1,3},{2,0},{3,1},{4,6},{5,7},{6,4},{7,5}} | collective-permute-start | bytes 786440 | tf_op jit(solution)/shard_map/ppermute | solution.py:627
  168.8 28.7 %collective-permute-start.1 = (f32[2,128,256]{2,1,0:T(8,128)}, f32[2,128,256]{2,1,0:T(8,128)}, u32[]{:S(2)}, u32[]{:S(2)}) collective-permute-start(f32[2,128,256]{2,1,0:T(8,128)} %get-tuple-element.25), channel_id=1, source_target_pairs={{0,4},{1,5},{2,6},{3,7},{4,0},{5,1},{6,2},{7,3}} | collective-permute-start | bytes 786440 | tf_op jit(solution)/shard_map/ppermute | solution.py:627
  170.3 60.8 %collective-permute-start.2 = (f32[6,128,512]{2,1,0:T(8,128)}, f32[6,128,512]{2,1,0:T(8,128)}, u32[]{:S(2)}, u32[]{:S(2)}) collective-permute-start(f32[6,128,512]{2,1,0:T(8,128)} %get-tuple-element.32), channel_id=1, source_target_pairs={{0,2},{1,3},{2,0},{3,1},{4,6},{5,7},{6,4},{7,5}} | collective-permute-start | bytes 4718600 | tf_op jit(solution)/shard_map/ppermute | solution.py:627
  170.8 60.3 %collective-permute-start.3 = (f32[6,128,512]{2,1,0:T(8,128)}, f32[6,128,512]{2,1,0:T(8,128)}, u32[]{:S(2)}, u32[]{:S(2)}) collective-permute-start(f32[6,128,512]{2,1,0:T(8,128)} %get-tuple-element.33), channel_id=1, source_target_pairs={{0,4},{1,5},{2,6},{3,7},{4,0},{5,1},{6,2},{7,3}} | collective-permute-start | bytes 4718600 | tf_op jit(solution)/shard_map/ppermute | solution.py:627
  172.3 71.9 %collective-permute-start.4 = (f32[6,128,512]{2,1,0:T(8,128)}, f32[6,128,512]{2,1,0:T(8,128)}, u32[]{:S(2)}, u32[]{:S(2)}) collective-permute-start(f32[6,128,512]{2,1,0:T(8,128)} %get-tuple-element.35), channel_id=1, source_target_pairs={{0,4},{1,5},{2,6},{3,7},{4,0},{5,1},{6,2},{7,3}} | collective-permute-start | bytes 4718600 | tf_op jit(solution)/shard_map/ppermute | solution.py:627
  177.4 66.7 %collective-permute-start.5 = (f32[6,128,512]{2,1,0:T(8,128)}, f32[6,128,512]{2,1,0:T(8,128)}, u32[]{:S(2)}, u32[]{:S(2)}) collective-permute-start(f32[6,128,512]{2,1,0:T(8,128)} %get-tuple-element.36), channel_id=1, source_target_pairs={{0,2},{1,3},{2,0},{3,1},{4,6},{5,7},{6,4},{7,5}} | collective-permute-start | bytes 4718600 | tf_op jit(solution)/shard_map/ppermute | solution.py:627
  200.1 26.7 %collective-permute-start.6 = (f32[4,128,256]{2,1,0:T(8,128)}, f32[4,128,256]{2,1,0:T(8,128)}, u32[]{:S(2)}, u32[]{:S(2)}) collective-permute-start(f32[4,128,256]{2,1,0:T(8,128)} %pad_maximum_fusion.sum_ref.mine_ref), channel_id=1, source_target_pairs={{0,1},{1,0},{2,3},{3,2},{4,5},{5,4},{6,7},{7,6}} | collective-permute-start | bytes 1572872 | tf_op jit(solution)/shard_map/ppermute | solution.py:627

commit v3 on v2

--- a/solution.py
+++ b/solution.py
@@ -27,7 +27,10 @@
     return pl.ds(pl.multiple_of(chunk * CHUNK, CHUNK), CHUNK)
 
 
-def attend_chunk(chunk, n_heads, scale, q_ref, do_ref, k_ref, v_ref, put, dk_ref, dv_ref):
+LOG2E = 1.4426950408889634
+
+
+def attend_chunk(chunk, n_heads, scale, q_ref, do_ref, k_ref, v_ref, put, dkt_ref, dvt_ref):
     for last in range(q_ref.shape[0] // CHUNK):
 
         @pl.when(chunk == last)
@@ -35,30 +38,34 @@
             span = (last + 1) * CHUNK
             rows = pl.ds(last * CHUNK, CHUNK)
 
-            def head(h, carry):
-                cols = pl.ds(pl.multiple_of(h * BLK, BLK), BLK)
-                q = q_ref[rows, cols]
-                d_out = do_ref[rows, cols]
+            def pair(j, carry):
                 keys = k_ref[:span, :]
                 vals = v_ref[:span, :]
-                s = mm(q, keys, 1, 1) * scale
                 row = lax.broadcasted_iota(jnp.int32, (CHUNK, CHUNK), 0)
                 col = lax.broadcasted_iota(jnp.int32, (CHUNK, CHUNK), 1)
-                s_diag = jnp.where(row >= col, s[:, span - CHUNK :], -jnp.inf)
-                s = s_diag if last == 0 else jnp.concatenate([s[:, : span - CHUNK], s_diag], axis=1)
-                e = jnp.exp(s - jnp.max(s, axis=1, keepdims=True))
-                p = e * (1.0 / jnp.sum(e, axis=1, keepdims=True))
-                pb = p.astype(BF16)
-                o = mm(pb, vals, 1, 0).astype(BF16)
-                delta = jnp.sum(d_out.astype(F32) * o.astype(F32), axis=1, keepdims=True)
-                ds = (p * (mm(d_out, vals, 1, 1) - delta)).astype(BF16)
-                dq = (mm(ds, keys, 1, 0) * scale).astype(BF16)
-                put(h, o, dq)
-                dk_ref[:span, :] += mm(ds, q, 0, 0)
-                dv_ref[:span, :] += mm(pb, d_out, 0, 0)
+                got = []
+                for h in (2 * j, 2 * j + 1):
+                    cols = pl.ds(pl.multiple_of(h * BLK, BLK), BLK)
+                    q = q_ref[rows, cols]
+                    d_out = do_ref[rows, cols]
+                    s = mm(q, keys, 1, 1)
+                    s_diag = jnp.where(row >= col, s[:, span - CHUNK :], -jnp.inf)
+                    s = s_diag if last == 0 else jnp.concatenate([s[:, : span - CHUNK], s_diag], axis=1)
+                    e = jnp.exp2((s - jnp.max(s, axis=1, keepdims=True)) * (scale * LOG2E))
+                    p = e * (1.0 / jnp.sum(e, axis=1, keepdims=True))
+                    pb = p.astype(BF16)
+                    o = mm(pb, vals, 1, 0).astype(BF16)
+                    delta = jnp.sum(d_out.astype(F32) * o.astype(F32), axis=1, keepdims=True)
+                    ds = (p * (mm(d_out, vals, 1, 1) - delta)).astype(BF16)
+                    dq = (mm(ds, keys, 1, 0) * scale).astype(BF16)
+                    put(h, o, dq)
+                    got.append((q, d_out, pb, ds))
+                q2, do2, pb2, ds2 = (jnp.concatenate(both, axis=0) for both in zip(*got))
+                dkt_ref[:, :span] += mm(q2, ds2, 0, 0)
+                dvt_ref[:, :span] += mm(do2, pb2, 0, 0)
                 return carry
 
-            lax.fori_loop(0, n_heads, head, 0)
+            lax.fori_loop(0, n_heads // 2, pair, 0)
 
 
 def front_kernel(
@@ -67,7 +74,7 @@
     xf_ref, dyf_ref, wqs_ref, pd_ref, r_ref, pxa_ref, pxb_ref, pya_ref, pyb_ref, poa_ref, pob_ref,
     of_ref, dqf_ref, kvo_ref, kx0_ref, kx1_ref, ky0_ref, ky1_ref,
     xb, yb, wq, wkv, wo, q_ref, do_ref, o_ref, dq_ref, k_ref, v_ref, dk_ref, dv_ref,
-    wt, pt, rt, got_q, dkv, got_kv, kvs,
+    pt, rt, got_q, dkv, got_kv, kvs,
     send_sem, recv_sem, wsem, lsem, osem, gq_send, gq_recv, gkv_send, gkv_recv,
     r_send, r_recv, kn_send, kn_recv, wt_sem, pt_sem, rt_sem, att_sem,
 ):
@@ -81,6 +88,7 @@
     pl.semaphore_wait(barrier, 3)
 
     bufs = (xb, yb)
+    n_w = wk_ref.shape[0]
     srcs = (x_ref, dy_ref)
     outs = (xf_ref, dyf_ref)
     counts = [0, 0]
@@ -115,8 +123,8 @@
     loads = [
         pltpu.make_async_copy(x_ref, xb.at[me], lsem.at[0]),
         pltpu.make_async_copy(wq_ref, wq, lsem.at[1]),
-        pltpu.make_async_copy(wk_ref, wkv.at[0], lsem.at[2]),
-        pltpu.make_async_copy(wv_ref, wkv.at[1], lsem.at[3]),
+        pltpu.make_async_copy(wk_ref, wkv.at[pl.ds(0, n_w)], lsem.at[2]),
+        pltpu.make_async_copy(wv_ref, wkv.at[pl.ds(n_w, n_w)], lsem.at[3]),
         pltpu.make_async_copy(dy_ref, yb.at[me], lsem.at[4]),
         pltpu.make_async_copy(wo_ref, wo, lsem.at[5]),
     ]
@@ -131,8 +139,6 @@
     dk_ref[...] = jnp.zeros_like(dk_ref)
     dv_ref[...] = jnp.zeros_like(dv_ref)
 
-    writes = []
-
     def chunk_of(p):
         return jnp.bitwise_xor(chip, p)
 
@@ -141,14 +147,14 @@
 
     def write_out(t, p):
         chunk = chunk_of(p)
-        for i in range(2):
-            copy = pltpu.make_async_copy(
+        return [
+            pltpu.make_async_copy(
                 bufs[t].at[2 * chunk + i],
                 outs[t].at[pl.ds(pl.multiple_of((2 * chunk + i) * BLK, BLK), BLK)],
                 osem.at[t, p, i],
             )
-            copy.start()
-            writes.append(copy)
+            for i in range(2)
+        ]
 
     def project(p):
         chunk = chunk_of(p)
@@ -161,10 +167,12 @@
             return carry
 
         lax.fori_loop(0, n_heads // 2, pair, 0)
-        kv = mm(x, jnp.concatenate([wkv[0], wkv[1]], axis=1), 1, 0).astype(BF16)
+        wide_kv = [wkv[g * n_w : (g + 1) * n_w].reshape(n_w * TILE, BLK) for g in range(2)]
+        kv = mm(x, jnp.concatenate(wide_kv, axis=1), 1, 0).astype(BF16)
         k_ref[rows, :] = kv[:, :BLK]
         v_ref[rows, :] = kv[:, BLK:]
-        write_out(0, p)
+        for copy in write_out(0, p):
+            copy.start()
 
     def project_out(p):
         chunk = chunk_of(p)
@@ -177,7 +185,8 @@
             return carry
 
         lax.fori_loop(0, n_heads // 2, pair, 0)
-        write_out(1, p)
+        for copy in write_out(1, p):
+            copy.start()
 
     def both(t, mask):
         arrive(t, mask, 0)
@@ -207,12 +216,24 @@
     def give_kv(p):
         return remote(dkv.at[block_rows(p, 1 - core)], got_kv.at[p], gkv_send.at[p], gkv_recv.at[p], SIB)
 
-    tile = wt.shape[2]
+    tile = wkv.shape[1]
     steps = pd_ref.shape[1]
 
     def w_load(side, i):
         col = pl.multiple_of((side * steps + i) * tile, tile)
-        return pltpu.make_async_copy(wqs_ref.at[:, pl.ds(col, tile), :], wt.at[side], wt_sem.at[side])
+        slot = lax.rem(2 * i + side, W_SLOTS)
+        return pltpu.make_async_copy(wqs_ref.at[:, pl.ds(col, tile), :], wkv.at[pl.ds(slot * n_heads, n_heads)], wt_sem.at[slot])
+
+    def w_ahead(side, i):
+        t = 2 * i + side + W_SLOTS - 1
+
+        @pl.when(t < 2 * steps)
+        def _():
+            w_load(lax.rem(t, 2), t // 2).start()
+
+    def w_first():
+        for t in range(W_SLOTS - 1):
+            w_load(t % 2, t // 2).start()
 
     def product(groups, side, i):
         col = pl.multiple_of((side * steps + i) * tile, tile)
@@ -224,7 +245,7 @@
             axis=1,
         )
         rhs = jnp.concatenate(
-            [wq[h, pl.ds(col, tile), :] for h in range(n_heads)] + [wt[side, h] for h in range(n_heads)], axis=1
+            [wq[h, pl.ds(col, tile), :] for h in range(n_heads)] + [wkv[lax.rem(2 * i + side, W_SLOTS) * n_heads + h] for h in range(n_heads)], axis=1
         )
         return mm(lhs, rhs, 1, 1)
 
@@ -269,25 +290,20 @@
         else:
             project_out(3)
 
-    attend_rows(3)
-    give_q(3).start()
-    w_copy.wait()
-    for side in range(2):
-        w_load(side, 0).start()
-    for copy in att_out(3):
-        copy.start()
-    give_q(3).wait_recv()
-
     def pd_write(side, i):
         return pltpu.make_async_copy(pt.at[side, pl.ds(0, BLK)], pd_ref.at[side, i], pt_sem.at[side, 0])
 
     def round1(side, i):
-        mask = (X_NBR, Y_NBR)[side]
-        return remote(pd_ref.at[side, i], r_ref.at[side, i], r_send.at[side, i], r_recv.at[side, i], mask)
+        return pltpu.make_async_remote_copy(
+            src_ref=pd_ref.at[side, i], dst_ref=r_ref.at[side, i],
+            send_sem=r_send.at[side, i], recv_sem=r_recv.at[side, i],
+            device_id={"tp": jnp.bitwise_xor(me, X_NBR * (1 + side))}, device_id_type=MESH,
+        )
 
     def pd_step(i, carry):
         for side in range(2):
             w_load(side, i).wait()
+            w_ahead(side, i)
             res = product((3,), side, i)
 
             @pl.when(i > 0)
@@ -298,45 +314,60 @@
             pt[side, :BLK] = res
             pd_write(side, i).start()
 
-            @pl.when(i < steps - 1)
-            def _(side=side):
-                w_load(side, i + 1).start()
-
         return carry
 
-    lax.fori_loop(0, steps, pd_step, 0)
-    for side in range(2):
-        pd_write(side, steps - 1).wait()
-        round1(side, steps - 1).start()
-        w_load(side, 0).start()
-
-    arrive(1, X_NBR, 1)
-    send(1, partner[X_NBR], 1, SIB)
-    arrive(1, Y_NBR, 0)
-    send(1, partner[Y_NBR], 0, SIB)
-    both(1, X_NBR ^ SIB)
-    project_out(1)
-    both(1, Y_NBR ^ SIB)
-    project_out(2)
-
-    def rest(i, carry):
-        p = lax.rem(i + 1, 3)
+    def late(i):
+        block, half = ((partner[X_NBR], 1), (partner[Y_NBR], 0))[i]
+        here = part(1, block, half)
+        return remote(here, here, send_sem.at[1, counts[1] + i], recv_sem.at[1, block, half], SIB)
+
+    def rows_step(i, carry):
+        p = 3 - i
         attend_rows(p)
         give_q(p).start()
         for copy in att_out(p):
             copy.start()
+
+        @pl.when(i == 0)
+        def _():
+            w_copy.wait()
+            w_first()
+            give_q(3).wait_recv()
+            lax.fori_loop(0, steps, pd_step, 0)
+            for side in range(2):
+                pd_write(side, steps - 1).wait()
+                round1(side, steps - 1).start()
+            w_first()
+            arrive(1, X_NBR, 1)
+            late(0).start()
+            arrive(1, Y_NBR, 0)
+            late(1).start()
+            both(1, X_NBR ^ SIB)
+            project_out(1)
+            both(1, Y_NBR ^ SIB)
+            project_out(2)
+
         return carry
 
-    lax.fori_loop(0, 3, rest, 0)
-    dkv[:, :BLK] = (dk_ref[...] * scale).astype(BF16)
-    dkv[:, BLK:] = dv_ref[...].astype(BF16)
+    lax.fori_loop(0, 4, rows_step, 0)
+    dkv[:, :BLK] = (dk_ref[...].T * scale).astype(BF16)
+    dkv[:, BLK:] = dv_ref[...].T.astype(BF16)
     for p in range(3):
         give_q(p).wait_recv()
     for p in range(4):
         give_kv(p).start()
 
     def r_load(side, i):
-        return pltpu.make_async_copy(r_ref.at[side, i], rt.at[side], rt_sem.at[side])
+        slot = lax.rem(2 * i + side, R_SLOTS)
+        return pltpu.make_async_copy(r_ref.at[side, i], rt.at[slot], rt_sem.at[slot])
+
+    def r_ahead(side, i):
+        t = 2 * i + side + R_SLOTS - 1
+
+        @pl.when(t < 2 * steps)
+        def _():
+            round1(lax.rem(t, 2), t // 2).wait_recv()
+            r_load(lax.rem(t, 2), t // 2).start()
 
     groups = (1, 2, 0)
     targets = ((pxa_ref, pya_ref, poa_ref), (pxb_ref, pyb_ref, pob_ref))
@@ -349,9 +380,9 @@
 
     def p_step(i, carry):
         for side in range(2):
-            round1(side, i).wait_recv()
-            r_load(side, i).start()
             w_load(side, i).wait()
+            w_ahead(side, i)
+            r_ahead(side, i)
             res = product(groups, side, i)
 
             @pl.when(i > 0)
@@ -363,16 +394,15 @@
             add = 1 - side
             for g in range(3):
                 rows = res[g * BLK : (g + 1) * BLK]
-                pt[side, g * BLK : (g + 1) * BLK] = rows + rt[side] if g == add else rows
+                pt[side, g * BLK : (g + 1) * BLK] = rows + rt[lax.rem(2 * i + side, R_SLOTS)] if g == add else rows
             for copy in p_writes(side, i):
                 copy.start()
 
-            @pl.when(i < steps - 1)
-            def _(side=side):
-                w_load(side, i + 1).start()
-
         return carry
 
+    for t in range(R_SLOTS - 1):
+        round1(t % 2, t // 2).wait_recv()
+        r_load(t % 2, t // 2).start()
     for p in range(4):
         give_kv(p).wait_recv()
         kvs[p] = dkv[block_rows(p, core), :].astype(F32) + got_kv[p].astype(F32)
@@ -392,6 +422,8 @@
             copy.wait()
     for copy in sends:
         copy.wait_send()
+    for i in range(2):
+        late(i).wait_send()
     for p in range(4):
         give_q(p).wait_send()
         give_kv(p).wait_send()
@@ -403,11 +435,15 @@
     for copy in near:
         copy.wait()
     kv_out.wait()
-    for copy in writes:
-        copy.wait()
+    for t in range(2):
+        for p in range(4):
+            for copy in write_out(t, p):
+                copy.wait()
 
 
 TILE = 512
+W_SLOTS = 4
+R_SLOTS = 4
 
 
 def front(x_blk, dy_blk, wq, wk, wv, wo, n_dev, scale):
@@ -433,7 +469,7 @@
             pltpu.VMEM((n_dev, BLK, dim), BF16),
             pltpu.VMEM((n_dev, BLK, dim), BF16),
             pltpu.VMEM(wq.shape, BF16),
-            pltpu.VMEM((2, dim, hd), BF16),
+            pltpu.VMEM((max(2 * dim // TILE, W_SLOTS * n_heads), TILE, hd), BF16),
             pltpu.VMEM(wo.shape, BF16),
             pltpu.VMEM((tokens, wide), BF16),
             pltpu.VMEM((tokens, wide), BF16),
@@ -441,11 +477,10 @@
             pltpu.VMEM((tokens, wide), BF16),
             pltpu.VMEM((tokens, hd), BF16),
             pltpu.VMEM((tokens, hd), BF16),
-            pltpu.VMEM((tokens, hd), F32),
-            pltpu.VMEM((tokens, hd), F32),
-            pltpu.VMEM((2, n_heads, TILE, hd), BF16),
+            pltpu.VMEM((hd, tokens), F32),
+            pltpu.VMEM((hd, tokens), F32),
             pltpu.VMEM((2, 3 * BLK, TILE), F32),
-            pltpu.VMEM((2, BLK, TILE), F32),
+            pltpu.VMEM((R_SLOTS, BLK, TILE), F32),
             pltpu.VMEM((4, BLK, wide), BF16),
             pltpu.VMEM((tokens, 2 * hd), BF16),
             pltpu.VMEM((4, BLK, 2 * hd), BF16),
@@ -453,11 +488,11 @@
             sem((2, 14)), sem((2, n_dev, 2)), sem((2,)), sem((6,)), sem((2, 4, 2)),
             sem((4,)), sem((4,)), sem((4,)), sem((4,)),
             sem((2, steps)), sem((2, steps)), sem((2, 2)), sem((2, 2)),
-            sem((2,)), sem((2, 3)), sem((2,)), sem((4, 2)),
+            sem((W_SLOTS,)), sem((2, 3)), sem((R_SLOTS,)), sem((4, 2)),
         ],
         compiler_params=pltpu.CompilerParams(collective_id=0, has_side_effects=True, vmem_limit_bytes=FULL),
         name="front",
-    )(x_blk, dy_blk, wq, wk, wv, wo)
+    )(x_blk, dy_blk, wq, wk.reshape(-1, TILE, hd), wv.reshape(-1, TILE, hd), wo)
 
 
 def dwo_kernel(o_ref, dy_ref, out_ref, o_t):
@@ -563,18 +598,18 @@
     )(me, mine, other, x_full)
 
 
-def kvdx_kernel(sum_ref, wka_ref, wkb_ref, wva_ref, wvb_ref, pa_ref, pb_ref, oa_ref, ob_ref):
+def kvdx_kernel(sum_ref, wka_ref, wkb_ref, wva_ref, wvb_ref, pa_ref, pb_ref, ra_ref, rb_ref, oa_ref, ob_ref):
     pieces = split3(sum_ref[0])
-    for wk_ref, wv_ref, p_ref, o_ref in (
-        (wka_ref, wva_ref, pa_ref, oa_ref),
-        (wkb_ref, wvb_ref, pb_ref, ob_ref),
+    for wk_ref, wv_ref, p_ref, r_ref, o_ref in (
+        (wka_ref, wva_ref, pa_ref, ra_ref, oa_ref),
+        (wkb_ref, wvb_ref, pb_ref, rb_ref, ob_ref),
     ):
         w = jnp.concatenate([wk_ref[...], wv_ref[...]], axis=1)
         res = mm(jnp.concatenate(pieces, axis=0), w, 1, 1)
-        o_ref[...] = p_ref[...] + (res[:BLK] + res[BLK : 2 * BLK] + res[2 * BLK :])
-
-
-def kv_dx(total, wk, wv, pa, pb):
+        o_ref[...] = (p_ref[...] + r_ref[...]) + (res[:BLK] + res[BLK : 2 * BLK] + res[2 * BLK :])
+
+
+def kv_dx(total, wk, wv, pa, pb, ra, rb):
     dim, hd = wk.shape
     steps, _, tile = pa.shape
     w_lo = pl.BlockSpec((tile, hd), lambda j: (j, 0))
@@ -584,38 +619,42 @@
         kvdx_kernel,
         grid=(steps,),
         out_shape=(jax.ShapeDtypeStruct(pa.shape, F32),) * 2,
-        in_specs=[pl.BlockSpec((1,) + total.shape[1:], lambda j: (0, 0, 0)), w_lo, w_hi, w_lo, w_hi, col, col],
+        in_specs=[pl.BlockSpec((1,) + total.shape[1:], lambda j: (0, 0, 0)), w_lo, w_hi, w_lo, w_hi, col, col, col, col],
         out_specs=(col, col),
         compiler_params=pltpu.CompilerParams(vmem_limit_bytes=FULL),
         cost_estimate=pl.CostEstimate(flops=12 * BLK * dim * hd, bytes_accessed=10 * 2**20, transcendentals=0),
         name="kv_dx",
-    )(total, wk, wk, wv, wv, pa, pb)
-
-
-def dx_sum_kernel(steps, a0, a1, a2, b0, b1, b2, out_ref):
+    )(total, wk, wk, wv, wv, pa, pb, ra, rb)
+
+
+GROUP = 3
+
+
+def dx_sum_kernel(groups, a0, a1, b0, b1, out_ref):
     j = pl.program_id(0)
-
-    @pl.when(j < steps)
-    def _():
-        out_ref[...] = ((a0[...] + a1[...]) + a2[...]).astype(BF16)
-
-    @pl.when(j >= steps)
-    def _():
-        out_ref[...] = ((b0[...] + b1[...]) + b2[...]).astype(BF16)
+    tile = a0.shape[2]
+
+    def add(x, y):
+        for g in range(GROUP):
+            out_ref[:, g * tile : (g + 1) * tile] = (x[g] + y[g]).astype(BF16)
+
+    pl.when(j < groups)(lambda: add(a0, a1))
+    pl.when(j >= groups)(lambda: add(b0, b1))
 
 
 def dx_sum(a_terms, b_terms):
     steps, _, tile = a_terms[0].shape
-    a_spec = pl.BlockSpec((None, BLK, tile), lambda j: (jnp.minimum(j, steps - 1), 0, 0))
-    b_spec = pl.BlockSpec((None, BLK, tile), lambda j: (jnp.maximum(j - steps, 0), 0, 0))
+    groups = steps // GROUP
+    a_spec = pl.BlockSpec((GROUP, BLK, tile), lambda j: (jnp.minimum(j, groups - 1), 0, 0))
+    b_spec = pl.BlockSpec((GROUP, BLK, tile), lambda j: (jnp.maximum(j - groups, 0), 0, 0))
     return pl.pallas_call(
-        functools.partial(dx_sum_kernel, steps),
-        grid=(2 * steps,),
+        functools.partial(dx_sum_kernel, groups),
+        grid=(2 * groups,),
         out_shape=jax.ShapeDtypeStruct((BLK, 2 * steps * tile), BF16),
-        in_specs=[a_spec] * 3 + [b_spec] * 3,
-        out_specs=pl.BlockSpec((BLK, tile), lambda j: (0, j)),
+        in_specs=[a_spec] * 2 + [b_spec] * 2,
+        out_specs=pl.BlockSpec((BLK, GROUP * tile), lambda j: (0, j)),
         compiler_params=pltpu.CompilerParams(vmem_limit_bytes=FULL),
-        cost_estimate=pl.CostEstimate(flops=2**20, bytes_accessed=12 * 2**20, transcendentals=0),
+        cost_estimate=pl.CostEstimate(flops=2**20, bytes_accessed=8 * 2**20, transcendentals=0),
         name="dx_sum",
     )(*a_terms, *b_terms)
 
@@ -650,9 +689,9 @@
         total = jnp.stack([kvs[p] + kv_x[p ^ 1] + kv_y[p ^ 2] + kv_d[p ^ 3] for p in range(4)])
         other = swap(total, SIB)
         dwq = grad_wq(xf, dq)
-        base_a, base_b = kv_dx(total, wk, wv, po_a, po_b)
+        base_a, base_b = kv_dx(total, wk, wv, po_a, po_b, a2, b2)
         dwk, dwv = grad_kv(me, total, other, xf, n_dev)
-        dx = dx_sum((base_a, a2, a3), (base_b, b2, b3))
+        dx = dx_sum((base_a, a3), (base_b, b3))
         return dx, jnp.transpose(dwq, (1, 0, 2)), dwo, dwk, dwv
 
     tok_spec = P(("dp", "tp"))

time: 255 us -> 239 us (0.937)
  Pallas kernels: 227 us -> 211 us
    pallas_call x1, Pallas kernels: 168 us -> 155 us  [front(): pl.pallas_call(functools.partial(front_kernel, n_heads, scale), out_shape...]
    pallas_call x1, Pallas kernels: 9.02 us -> 5 us  [dx_sum(): pl.pallas_call(functools.partial(dx_sum_kernel, groups), grid=(2 * groups...]
  transfers between devices with their start and end apart: 7 -> 7, of which waited for: 2 -> 2; matrix products, arithmetic and copies ran while one was open for 1% -> 1% of each run, Pallas kernels for 20% -> 21%
where the time goes in v3:
time: 239 us; the launch traced here: 237 us
  Pallas kernels  211 us (88%)
  waiting for transfers between devices  15.4 us (6%)
  starting transfers between devices  7.42 us (3%)
  other arithmetic  2.57 us (1%)
    pallas_call x1, Pallas kernels, front(): pl.pallas_call(functools.partial(front_kernel, n_heads, scale), out_shape...  155 us
    pallas_call x1, Pallas kernels, grad_wo(): pl.pallas_call(dwo_kernel, grid=(dim // tile,), out_shape=jax.ShapeDtypeS...  19.6 us
    pallas_call x1, Pallas kernels, grad_wq(): pl.pallas_call(dwq_kernel, grid=(dim // tile,), out_shape=jax.ShapeDtypeS...  19.5 us
    ppermute x7, waiting for transfers between devices, swap(): return lax.ppermute(a, 'tp', [(i, i ^ mask) for i in range(n_dev)])  15.4 us
    pallas_call x1, Pallas kernels, kv_dx(): pl.pallas_call(kvdx_kernel, grid=(steps,), out_shape=(jax.ShapeDtypeStruc...  7.5 us
    ppermute x7, starting transfers between devices, swap(): return lax.ppermute(a, 'tp', [(i, i ^ mask) for i in range(n_dev)])  7.42 us
    pallas_call x1, Pallas kernels, dx_sum(): pl.pallas_call(functools.partial(dx_sum_kernel, groups), grid=(2 * groups...  5 us
  transfers between devices with their start and end apart: 7, of which 2 were waited for; matrix products, arithmetic and copies ran while one was open for 1% of the time, Pallas kernels for 21%

profile of v3, /device:TPU:0, one launch (start us, length us, event | category | flops | bytes accessed | tf_op | source)
XLA Modules:
  0.0 237.4 jit_solution(1489538804344358889)
XLA Ops:
  0.6 155.4 %front.1 = (bf16[1024,6144]{1,0:T(8,128)(2,1)}, bf16[1024,6144]{1,0:T(8,128)(2,1)}, bf16[6,6144,128]{2,1,0:T(8,128)(2,1)}, f32[2,6,128,512]{3,2,1,0:T(8,128)}, f...) custom-call(bf16[128,6144]{1,0:T(8,128)(2,1)} %x_ref.1, ...), custom_call_target="tpu_custom_call" | custom-call | tf_op jit(solution)/shard_map/front/pallas_call | solution.py:457
  156.1 1.5 collective-permute-start
  157.6 0.6 collective-permute-start.1
  158.1 1.9 collective-permute-start.2
  160.0 0.1 collective-permute-start.3
  160.1 1.9 collective-permute-start.4
  162.0 3.2 %collective-permute-done = f32[2,128,256]{2,1,0:T(8,128)} collective-permute-done((f32[2,128,256]{2,1,0:T(8,128)}, f32[2,128,256]{2,1,0:T(8,128)}, u32[]{:S(2)}, u32[]{:S(2)}) %collective-permute-start) | collective-permute-done | bytes 262176 | tf_op jit(solution)/shard_map/ppermute | solution.py:666
  165.3 1.5 collective-permute-start.5
  166.7 19.5 %grad_wq.1 = f32[6,6144,128]{2,1,0:T(8,128)} custom-call(bf16[1024,6144]{1,0:T(8,128)(2,1)} %get-tuple-element.37.x_ref, bf16[1024,768]{1,0:T(8,128)(2,1)} %get-tuple-element.38.dq_ref), custom_call_target="tpu_custom_call" | custom-call | flops 9663676416 | bytes 31457280 | tf_op jit(solution)/shard_map/grad_wq/pallas_call | solution.py:539
  186.2 0.0 collective-permute-done.1
  186.2 1.7 slice_add_fusion.3
  188.0 0.8 pad_maximum_fusion.sum_ref.mine_ref
  188.8 0.0 collective-permute-start.6
  188.8 19.6 %grad_wo.1 = f32[6,128,6144]{2,1,0:T(8,128)} custom-call(bf16[1024,768]{1,0:T(8,128)(2,1)} %get-tuple-element.39.o_ref, bf16[1024,6144]{1,0:T(8,128)(2,1)} %get-tuple-element.40.dy_ref), custom_call_target="tpu_custom_call" | custom-call | flops 9663676416 | bytes 31457280 | tf_op jit(solution)/shard_map/grad_wo/pallas_call | solution.py:513
  208.5 0.0 collective-permute-done.6.other_ref
  208.5 4.4 %grad_kv.1 = (f32[768,128]{1,0:T(8,128)}, f32[768,128]{1,0:T(8,128)}) custom-call(s32[1]{0:T(128)} %bitcast.6.me_ref, f32[4,128,256]{2,1,0:T(8,128)} %pad_maximum_fusion.sum_ref.mine_ref, f32[4,128,256]{2,1,0:T(8,128)} %collective-permute-done.6.other_ref, bf16[1024,6144]{1,0:T(8,128)(2,1)} %get-tuple-element.37.x_ref), custom_call_target="tpu_custom_call" | custom-call | flops 1207959552 | bytes 3145728 | tf_op jit(solution)/shard_map/grad_kv/pallas_call | solution.py:583
  212.8 0.0 collective-permute-done.2.ra_ref
  212.8 0.0 collective-permute-done.3.rb_ref
  212.8 7.5 %kv_dx.1 = (f32[6,128,512]{2,1,0:T(8,128)}, f32[6,128,512]{2,1,0:T(8,128)}) custom-call(f32[4,128,256]{2,1,0:T(8,128)} %pad_maximum_fusion.sum_ref.mine_ref, bf16[6144,128]{1,0:T(8,128)(2,1)} %bitcast.8, bf16[6144,128]{1,0:T(8,128)(2,1)} %bitcast.9, bf16[6144,128]{1,0:T(8,128)(2,1)} %bitcast.11, bf16[6144,128]{1,0:T(8,128)(2,1)} %bitcast.12, ...), custom_call_target="tpu_custom_call" | custom-call | flops 1207959552 | bytes 10485760 | tf_op jit(solution)/shard_map/kv_dx/pallas_call | solution.py:618
  220.3 12.1 %collective-permute-done.4.a1 = f32[6,128,512]{2,1,0:T(8,128)} collective-permute-done((f32[6,128,512]{2,1,0:T(8,128)}, f32[6,128,512]{2,1,0:T(8,128)}, u32[]{:S(2)}, u32[]{:S(2)}) %collective-permute-start.4) | collective-permute-done | bytes 1572896 | tf_op jit(solution)/shard_map/ppermute | solution.py:666
  232.4 0.0 collective-permute-done.5.b1
  232.4 5.0 %dx_sum.1 = bf16[128,6144]{1,0:T(8,128)(2,1)} custom-call(f32[6,128,512]{2,1,0:T(8,128)} %get-tuple-element.33.a0, f32[6,128,512]{2,1,0:T(8,128)} %collective-permute-done.4.a1, f32[6,128,512]{2,1,0:T(8,128)} %get-tuple-element.35.b0, f32[6,128,512]{2,1,0:T(8,128)} %collective-permute-done.5.b1), custom_call_target="tpu_custom_call" | custom-call | flops 1048576 | bytes 8388608 | tf_op jit(solution)/shard_map/dx_sum/pallas_call | solution.py:650
Async XLA Ops:
  156.1 9.2 %collective-permute-start = (f32[2,128,256]{2,1,0:T(8,128)}, f32[2,128,256]{2,1,0:T(8,128)}, u32[]{:S(2)}, u32[]{:S(2)}) collective-permute-start(f32[2,128,256]{2,1,0:T(8,128)} %get-tuple-element.26), channel_id=1, source_target_pairs={{0,2},{1,3},{2,0},{3,1},{4,6},{5,7},{6,4},{7,5}} | collective-permute-start | bytes 786440 | tf_op jit(solution)/shard_map/ppermute | solution.py:666
  157.6 28.7 %collective-permute-start.1 = (f32[2,128,256]{2,1,0:T(8,128)}, f32[2,128,256]{2,1,0:T(8,128)}, u32[]{:S(2)}, u32[]{:S(2)}) collective-permute-start(f32[2,128,256]{2,1,0:T(8,128)} %get-tuple-element.25), channel_id=1, source_target_pairs={{0,4},{1,5},{2,6},{3,7},{4,0},{5,1},{6,2},{7,3}} | collective-permute-start | bytes 786440 | tf_op jit(solution)/shard_map/ppermute | solution.py:666
  158.1 54.7 %collective-permute-start.2 = (f32[6,128,512]{2,1,0:T(8,128)}, f32[6,128,512]{2,1,0:T(8,128)}, u32[]{:S(2)}, u32[]{:S(2)}) collective-permute-start(f32[6,128,512]{2,1,0:T(8,128)} %get-tuple-element.31), channel_id=1, source_target_pairs={{0,2},{1,3},{2,0},{3,1},{4,6},{5,7},{6,4},{7,5}} | collective-permute-start | bytes 4718600 | tf_op jit(solution)/shard_map/ppermute | solution.py:666
  160.0 52.8 %collective-permute-start.3 = (f32[6,128,512]{2,1,0:T(8,128)}, f32[6,128,512]{2,1,0:T(8,128)}, u32[]{:S(2)}, u32[]{:S(2)}) collective-permute-start(f32[6,128,512]{2,1,0:T(8,128)} %get-tuple-element.32), channel_id=1, source_target_pairs={{0,4},{1,5},{2,6},{3,7},{4,0},{5,1},{6,2},{7,3}} | collective-permute-start | bytes 4718600 | tf_op jit(solution)/shard_map/ppermute | solution.py:666
  160.1 72.3 %collective-permute-start.4 = (f32[6,128,512]{2,1,0:T(8,128)}, f32[6,128,512]{2,1,0:T(8,128)}, u32[]{:S(2)}, u32[]{:S(2)}) collective-permute-start(f32[6,128,512]{2,1,0:T(8,128)} %get-tuple-element.34), channel_id=1, source_target_pairs={{0,4},{1,5},{2,6},{3,7},{4,0},{5,1},{6,2},{7,3}} | collective-permute-start | bytes 4718600 | tf_op jit(solution)/shard_map/ppermute | solution.py:666
  165.3 67.2 %collective-permute-start.5 = (f32[6,128,512]{2,1,0:T(8,128)}, f32[6,128,512]{2,1,0:T(8,128)}, u32[]{:S(2)}, u32[]{:S(2)}) collective-permute-start(f32[6,128,512]{2,1,0:T(8,128)} %get-tuple-element.36), channel_id=1, source_target_pairs={{0,2},{1,3},{2,0},{3,1},{4,6},{5,7},{6,4},{7,5}} | collective-permute-start | bytes 4718600 | tf_op jit(solution)/shard_map/ppermute | solution.py:666
  188.8 19.6 %collective-permute-start.6 = (f32[4,128,256]{2,1,0:T(8,128)}, f32[4,128,256]{2,1,0:T(8,128)}, u32[]{:S(2)}, u32[]{:S(2)}) collective-permute-start(f32[4,128,256]{2,1,0:T(8,128)} %pad_maximum_fusion.sum_ref.mine_ref), channel_id=1, source_target_pairs={{0,1},{1,0},{2,3},{3,2},{4,5},{5,4},{6,7},{7,6}} | collective-permute-start | bytes 1572872 | tf_op jit(solution)/shard_map/ppermute | solution.py:666

commit v4 on v3

--- a/solution.py
+++ b/solution.py
@@ -627,32 +627,45 @@
     )(total, wk, wk, wv, wv, pa, pb, ra, rb)
 
 
-GROUP = 3
-
-
-def dx_sum_kernel(groups, a0, a1, b0, b1, out_ref):
-    j = pl.program_id(0)
-    tile = a0.shape[2]
-
-    def add(x, y):
-        for g in range(GROUP):
-            out_ref[:, g * tile : (g + 1) * tile] = (x[g] + y[g]).astype(BF16)
-
-    pl.when(j < groups)(lambda: add(a0, a1))
-    pl.when(j >= groups)(lambda: add(b0, b1))
+def dx_sum_kernel(a0, a1, b0, b1, out_ref, terms, res, in_sem, out_sem):
+    steps, _, tile = a0.shape
+    sides = ((a0, a1), (b0, b1))
+
+    def load(side, i, n):
+        return pltpu.make_async_copy(sides[side][n].at[i], terms.at[side, n, i], in_sem.at[side, n, i])
+
+    def store(side, i):
+        cols = pl.ds((side * steps + i) * tile, tile)
+        return pltpu.make_async_copy(res.at[:, cols], out_ref.at[:, cols], out_sem.at[side, i])
+
+    order = [(side, i) for side in range(2) for i in range(steps)]
+    for side, i in order:
+        for n in range(2):
+            load(side, i, n).start()
+    for side, i in order:
+        for n in range(2):
+            load(side, i, n).wait()
+        at = (side * steps + i) * tile
+        res[:, at : at + tile] = (terms[side, 0, i] + terms[side, 1, i]).astype(BF16)
+        store(side, i).start()
+    for side, i in order:
+        store(side, i).wait()
 
 
 def dx_sum(a_terms, b_terms):
-    steps, _, tile = a_terms[0].shape
-    groups = steps // GROUP
-    a_spec = pl.BlockSpec((GROUP, BLK, tile), lambda j: (jnp.minimum(j, groups - 1), 0, 0))
-    b_spec = pl.BlockSpec((GROUP, BLK, tile), lambda j: (jnp.maximum(j - groups, 0), 0, 0))
+    steps, rows, tile = a_terms[0].shape
+    dim = 2 * steps * tile
     return pl.pallas_call(
-        functools.partial(dx_sum_kernel, groups),
-        grid=(2 * groups,),
-        out_shape=jax.ShapeDtypeStruct((BLK, 2 * steps * tile), BF16),
-        in_specs=[a_spec] * 2 + [b_spec] * 2,
-        out_specs=pl.BlockSpec((BLK, GROUP * tile), lambda j: (0, j)),
+        dx_sum_kernel,
+        out_shape=jax.ShapeDtypeStruct((rows, dim), BF16),
+        in_specs=[ANY] * 4,
+        out_specs=ANY,
+        scratch_shapes=[
+            pltpu.VMEM((2, 2, steps, rows, tile), F32),
+            pltpu.VMEM((rows, dim), BF16),
+            pltpu.SemaphoreType.DMA((2, 2, steps)),
+            pltpu.SemaphoreType.DMA((2, steps)),
+        ],
         compiler_params=pltpu.CompilerParams(vmem_limit_bytes=FULL),
         cost_estimate=pl.CostEstimate(flops=2**20, bytes_accessed=8 * 2**20, transcendentals=0),
         name="dx_sum",

time: 239 us -> 238 us (level)
  transfers between devices with their start and end apart: 7 -> 7, of which waited for: 2 -> 2; matrix products, arithmetic and copies ran while one was open for 1% -> 1% of each run, Pallas kernels for 21% -> 22%
where the time goes in v4:
time: 238 us; the launch traced here: 237 us
  Pallas kernels  211 us (89%)
  waiting for transfers between devices  15.4 us (6%)
  starting transfers between devices  7.42 us (3%)
  other arithmetic  2.57 us (1%)
    pallas_call x1, Pallas kernels, front(): pl.pallas_call(functools.partial(front_kernel, n_heads, scale), out_shape...  155 us
    pallas_call x1, Pallas kernels, grad_wo(): pl.pallas_call(dwo_kernel, grid=(dim // tile,), out_shape=jax.ShapeDtypeS...  19.6 us
    pallas_call x1, Pallas kernels, grad_wq(): pl.pallas_call(dwq_kernel, grid=(dim // tile,), out_shape=jax.ShapeDtypeS...  19.5 us
    ppermute x7, waiting for transfers between devices, swap(): return lax.ppermute(a, 'tp', [(i, i ^ mask) for i in range(n_dev)])  15.4 us
    pallas_call x1, Pallas kernels, kv_dx(): pl.pallas_call(kvdx_kernel, grid=(steps,), out_shape=(jax.ShapeDtypeStruc...  7.5 us
    ppermute x7, starting transfers between devices, swap(): return lax.ppermute(a, 'tp', [(i, i ^ mask) for i in range(n_dev)])  7.42 us
  transfers between devices with their start and end apart: 7, of which 2 were waited for; matrix products, arithmetic and copies ran while one was open for 1% of the time, Pallas kernels for 22%

profile of v4, /device:TPU:0, one launch (start us, length us, event | category | flops | bytes accessed | tf_op | source)
XLA Modules:
  0.0 236.7 jit_solution(17944032602813202385)
XLA Ops:
  0.6 155.4 %front.1 = (bf16[1024,6144]{1,0:T(8,128)(2,1)}, bf16[1024,6144]{1,0:T(8,128)(2,1)}, bf16[6,6144,128]{2,1,0:T(8,128)(2,1)}, f32[2,6,128,512]{3,2,1,0:T(8,128)}, f...) custom-call(bf16[128,6144]{1,0:T(8,128)(2,1)} %x_ref.1, ...), custom_call_target="tpu_custom_call" | custom-call | tf_op jit(solution)/shard_map/front/pallas_call | solution.py:457
  156.1 1.5 collective-permute-start
  157.6 0.6 collective-permute-start.1
  158.1 1.9 collective-permute-start.2
  160.0 0.1 collective-permute-start.3
  160.1 1.9 collective-permute-start.4
  162.0 3.2 %collective-permute-done = f32[2,128,256]{2,1,0:T(8,128)} collective-permute-done((f32[2,128,256]{2,1,0:T(8,128)}, f32[2,128,256]{2,1,0:T(8,128)}, u32[]{:S(2)}, u32[]{:S(2)}) %collective-permute-start) | collective-permute-done | bytes 262176 | tf_op jit(solution)/shard_map/ppermute | solution.py:679
  165.3 1.5 collective-permute-start.5
  166.7 19.5 %grad_wq.1 = f32[6,6144,128]{2,1,0:T(8,128)} custom-call(bf16[1024,6144]{1,0:T(8,128)(2,1)} %get-tuple-element.37.x_ref, bf16[1024,768]{1,0:T(8,128)(2,1)} %get-tuple-element.38.dq_ref), custom_call_target="tpu_custom_call" | custom-call | flops 9663676416 | bytes 31457280 | tf_op jit(solution)/shard_map/grad_wq/pallas_call | solution.py:539
  186.2 0.0 collective-permute-done.1
  186.2 1.7 slice_add_fusion.3
  188.0 0.8 pad_maximum_fusion.sum_ref.mine_ref
  188.8 0.0 collective-permute-start.6
  188.8 19.6 %grad_wo.1 = f32[6,128,6144]{2,1,0:T(8,128)} custom-call(bf16[1024,768]{1,0:T(8,128)(2,1)} %get-tuple-element.39.o_ref, bf16[1024,6144]{1,0:T(8,128)(2,1)} %get-tuple-element.40.dy_ref), custom_call_target="tpu_custom_call" | custom-call | flops 9663676416 | bytes 31457280 | tf_op jit(solution)/shard_map/grad_wo/pallas_call | solution.py:513
  208.5 0.0 collective-permute-done.6.other_ref
  208.5 4.4 %grad_kv.1 = (f32[768,128]{1,0:T(8,128)}, f32[768,128]{1,0:T(8,128)}) custom-call(s32[1]{0:T(128)} %bitcast.6.me_ref, f32[4,128,256]{2,1,0:T(8,128)} %pad_maximum_fusion.sum_ref.mine_ref, f32[4,128,256]{2,1,0:T(8,128)} %collective-permute-done.6.other_ref, bf16[1024,6144]{1,0:T(8,128)(2,1)} %get-tuple-element.37.x_ref), custom_call_target="tpu_custom_call" | custom-call | flops 1207959552 | bytes 3145728 | tf_op jit(solution)/shard_map/grad_kv/pallas_call | solution.py:583
  212.8 0.0 collective-permute-done.2.ra_ref
  212.8 0.0 collective-permute-done.3.rb_ref
  212.8 7.5 %kv_dx.1 = (f32[6,128,512]{2,1,0:T(8,128)}, f32[6,128,512]{2,1,0:T(8,128)}) custom-call(f32[4,128,256]{2,1,0:T(8,128)} %pad_maximum_fusion.sum_ref.mine_ref, bf16[6144,128]{1,0:T(8,128)(2,1)} %bitcast.8, bf16[6144,128]{1,0:T(8,128)(2,1)} %bitcast.9, bf16[6144,128]{1,0:T(8,128)(2,1)} %bitcast.11, bf16[6144,128]{1,0:T(8,128)(2,1)} %bitcast.12, ...), custom_call_target="tpu_custom_call" | custom-call | flops 1207959552 | bytes 10485760 | tf_op jit(solution)/shard_map/kv_dx/pallas_call | solution.py:618
  220.3 12.1 %collective-permute-done.4.a1 = f32[6,128,512]{2,1,0:T(8,128)} collective-permute-done((f32[6,128,512]{2,1,0:T(8,128)}, f32[6,128,512]{2,1,0:T(8,128)}, u32[]{:S(2)}, u32[]{:S(2)}) %collective-permute-start.4) | collective-permute-done | bytes 1572896 | tf_op jit(solution)/shard_map/ppermute | solution.py:679
  232.4 0.0 collective-permute-done.5.b1
  232.4 4.1 %dx_sum.1 = bf16[128,6144]{1,0:T(8,128)(2,1)} custom-call(f32[6,128,512]{2,1,0:T(8,128)} %get-tuple-element.33.a0, f32[6,128,512]{2,1,0:T(8,128)} %collective-permute-done.4.a1, f32[6,128,512]{2,1,0:T(8,128)} %get-tuple-element.35.b0, f32[6,128,512]{2,1,0:T(8,128)} %collective-permute-done.5.b1), custom_call_target="tpu_custom_call" | custom-call | flops 1048576 | bytes 8388608 | tf_op jit(solution)/shard_map/dx_sum/pallas_call | solution.py:658
Async XLA Ops:
  156.1 9.2 %collective-permute-start = (f32[2,128,256]{2,1,0:T(8,128)}, f32[2,128,256]{2,1,0:T(8,128)}, u32[]{:S(2)}, u32[]{:S(2)}) collective-permute-start(f32[2,128,256]{2,1,0:T(8,128)} %get-tuple-element.26), channel_id=1, source_target_pairs={{0,2},{1,3},{2,0},{3,1},{4,6},{5,7},{6,4},{7,5}} | collective-permute-start | bytes 786440 | tf_op jit(solution)/shard_map/ppermute | solution.py:679
  157.6 28.7 %collective-permute-start.1 = (f32[2,128,256]{2,1,0:T(8,128)}, f32[2,128,256]{2,1,0:T(8,128)}, u32[]{:S(2)}, u32[]{:S(2)}) collective-permute-start(f32[2,128,256]{2,1,0:T(8,128)} %get-tuple-element.25), channel_id=1, source_target_pairs={{0,4},{1,5},{2,6},{3,7},{4,0},{5,1},{6,2},{7,3}} | collective-permute-start | bytes 786440 | tf_op jit(solution)/shard_map/ppermute | solution.py:679
  158.1 54.7 %collective-permute-start.2 = (f32[6,128,512]{2,1,0:T(8,128)}, f32[6,128,512]{2,1,0:T(8,128)}, u32[]{:S(2)}, u32[]{:S(2)}) collective-permute-start(f32[6,128,512]{2,1,0:T(8,128)} %get-tuple-element.31), channel_id=1, source_target_pairs={{0,2},{1,3},{2,0},{3,1},{4,6},{5,7},{6,4},{7,5}} | collective-permute-start | bytes 4718600 | tf_op jit(solution)/shard_map/ppermute | solution.py:679
  160.0 52.8 %collective-permute-start.3 = (f32[6,128,512]{2,1,0:T(8,128)}, f32[6,128,512]{2,1,0:T(8,128)}, u32[]{:S(2)}, u32[]{:S(2)}) collective-permute-start(f32[6,128,512]{2,1,0:T(8,128)} %get-tuple-element.32), channel_id=1, source_target_pairs={{0,4},{1,5},{2,6},{3,7},{4,0},{5,1},{6,2},{7,3}} | collective-permute-start | bytes 4718600 | tf_op jit(solution)/shard_map/ppermute | solution.py:679
  160.1 72.3 %collective-permute-start.4 = (f32[6,128,512]{2,1,0:T(8,128)}, f32[6,128,512]{2,1,0:T(8,128)}, u32[]{:S(2)}, u32[]{:S(2)}) collective-permute-start(f32[6,128,512]{2,1,0:T(8,128)} %get-tuple-element.34), channel_id=1, source_target_pairs={{0,4},{1,5},{2,6},{3,7},{4,0},{5,1},{6,2},{7,3}} | collective-permute-start | bytes 4718600 | tf_op jit(solution)/shard_map/ppermute | solution.py:679
  165.3 67.2 %collective-permute-start.5 = (f32[6,128,512]{2,1,0:T(8,128)}, f32[6,128,512]{2,1,0:T(8,128)}, u32[]{:S(2)}, u32[]{:S(2)}) collective-permute-start(f32[6,128,512]{2,1,0:T(8,128)} %get-tuple-element.36), channel_id=1, source_target_pairs={{0,2},{1,3},{2,0},{3,1},{4,6},{5,7},{6,4},{7,5}} | collective-permute-start | bytes 4718600 | tf_op jit(solution)/shard_map/ppermute | solution.py:679
  188.8 19.6 %collective-permute-start.6 = (f32[4,128,256]{2,1,0:T(8,128)}, f32[4,128,256]{2,1,0:T(8,128)}, u32[]{:S(2)}, u32[]{:S(2)}) collective-permute-start(f32[4,128,256]{2,1,0:T(8,128)} %pad_maximum_fusion.sum_ref.mine_ref), channel_id=1, source_target_pairs={{0,1},{1,0},{2,3},{3,2},{4,5},{5,4},{6,7},{7,6}} | collective-permute-start | bytes 1572872 | tf_op jit(solution)/shard_map/ppermute | solution.py:679
